TPU v7x, 256 devices: a whole 4x4x8 slice. The times are simulated.
256 devices in a mesh: gx: 8 (over x_hi, y), gy: 4 (over x_lo, core), gz: 8 (over z).
Axes of the slice: x: 4 (x_hi: 2, x_lo: 2; x = x_hi * 2 + x_lo), y: 4, z: 8, core: 2. Of those that a mesh axis runs over, the one named last changes fastest.
Arguments:
- node_latents: bfloat16 [262144, 128], P(('gx', 'gy', 'gz')), may hold values from -300 to 300
- cluster_latents: bfloat16 [65536, 128], P(('gx', 'gy', 'gz')), may hold values from -6 to 6
- senders: int32 [8192, 128], P(('gx', 'gy', 'gz')), may hold values from 0 to 4095
- membership: int32 [262144], P(('gx', 'gy', 'gz')), may hold values from 0 to 255
- w_key: bfloat16 [128, 128], replicated, may hold values from -1 to 1
- w_value: bfloat16 [128, 128], replicated, may hold values from -0.5 to 0.5
- w_edge_in: bfloat16 [256, 128], replicated, may hold values from -0.375 to 0.375
- w_edge_out: bfloat16 [128, 128], replicated, may hold values from -0.5 to 0.5
- w_node_in: bfloat16 [512, 128], replicated, may hold values from -0.25 to 0.25
- w_node_out: bfloat16 [128, 128], replicated, may hold values from -0.5 to 0.5
- out_gain: float32 [128], replicated, may hold values from 0.5 to 1.5
Outputs:
- new_latents: bfloat16 [262144, 128], P(('gx', 'gy', 'gz'))
All inputs are finite; a program needn't handle non-finite values.
Results may differ from a plain program's by a relative error of at most 0.005.
Values may be sent and summed in bfloat16 or wider, within the bound.
A program may use at most 64 MiB of HBM per device.

v0:
```python
import jax
import jax.numpy as jnp
from jax import lax
from jax.sharding import PartitionSpec as P

BND = 512


NEG_FILL = -1e30


def from_everyone(shard, axis):
    size = lax.axis_size(axis)
    return lax.all_to_all(
        jnp.broadcast_to(shard[None], (size, *shard.shape)), axis, 0, 0, tiled=True
    )


def in_order(pieces, dim):
    pieces = jnp.moveaxis(pieces, 0, dim)
    lengths = pieces.shape
    return pieces.reshape(*lengths[:dim], lengths[dim] * lengths[dim + 1], *lengths[dim + 2 :])


def gather_directly(shard, axis, dim):
    pieces = from_everyone(shard, axis)
    return in_order(pieces, dim)


def in_one_piece(arrays, axis, dim, along):
    ends, at = ([], 0)
    for a in arrays[:-1]:
        at += a.shape[along]
        ends.append(at)
    both = jnp.concatenate(arrays, axis=along)
    return tuple(jnp.split(gather_directly(both, axis, dim), ends, axis=along))


def in_one_piece_2(arrays, axis, dim, along):
    ends, at = ([], 0)
    for a in arrays[:-1]:
        at += a.shape[along]
        ends.append(at)
    both = jnp.concatenate(arrays, axis=along)
    return tuple(jnp.split(lax.all_gather(both, axis, axis=dim, tiled=True), ends, axis=along))


def with_halo(shard, sides, width):
    edges = {}
    for axis, dim in sides:
        size, length = (lax.axis_size(axis), shard.shape[dim])
        up = [(i, (i + 1) % size) for i in range(size)]
        last = lax.slice_in_dim(shard, length - width, length, axis=dim)
        initial = lax.slice_in_dim(shard, 0, width, axis=dim)
        edges[dim] = (
            lax.ppermute(last, axis, up),
            lax.ppermute(initial, axis, [(b, a) for a, b in up]),
        )
    done = []
    for _, dim in sides:
        low, high = edges[dim]
        around = [(width, width) if d in done else (0, 0) for d in range(shard.ndim)]
        shard = jnp.concatenate([jnp.pad(low, around), shard, jnp.pad(high, around)], axis=dim)
        done.append(dim)
    return shard


def project(latent_rows, weight):
    return jnp.dot(latent_rows, weight, preferred_element_type=jnp.float32).astype(jnp.bfloat16)


def absorb_into(carry, key_rows, value_rows, queries):
    running_max, running_sum, weighted = carry
    scores = lax.dot_general(
        queries, key_rows, (((1,), (1,)), ((), ())), preferred_element_type=jnp.float32
    )
    scores = scores / jnp.sqrt(jnp.float32(queries.shape[1]))
    newest = jnp.maximum(running_max, jnp.max(scores, axis=1))
    exponent = jnp.exp(scores - newest[:, None])
    running_sum = jnp.sum(exponent, axis=1)
    weighted = jnp.dot(
        exponent.astype(jnp.bfloat16), value_rows, preferred_element_type=jnp.float32
    )
    return (newest, running_sum, weighted)


def on_device(
    node_latents,
    cluster_latents,
    senders,
    membership,
    w_key,
    w_value,
    w_edge_in,
    w_edge_out,
    w_node_in,
    w_node_out,
    out_gain,
):
    count, width = node_latents.shape
    start_carry = (
        jnp.full((count,), NEG_FILL, jnp.float32),
        jnp.zeros((count,), jnp.float32),
        jnp.zeros((count, width), jnp.float32),
    )
    key_rows = project(cluster_latents, w_key)
    value_rows = project(cluster_latents, w_value)

    def visit_pairs(carry, portion):
        return absorb_into(carry, portion[0], portion[1], node_latents)

    along_x = visit_pairs(start_carry, in_one_piece((key_rows, value_rows), "gx", 0, 1))
    along_y = visit_pairs(start_carry, in_one_piece_2((key_rows, value_rows), "gy", 0, 1))
    along_z = visit_pairs(start_carry, in_one_piece_2((key_rows, value_rows), "gz", 0, 1))
    pooled = (
        along_x[2] / along_x[1][:, None]
        + along_y[2] / along_y[1][:, None]
        + along_z[2] / along_z[1][:, None]
    )
    attended = (
        pooled * lax.rsqrt(jnp.mean(pooled * pooled, axis=1, keepdims=True) + 1e-06)
    ).astype(jnp.bfloat16)
    border = node_latents[:BND].reshape(1, 1, 1, BND, width)
    padded = with_halo(border, (("gx", 0), ("gy", 1), ("gz", 2)), 1)
    extended = jnp.concatenate(
        [
            node_latents,
            padded[0, 1, 1],
            padded[2, 1, 1],
            padded[1, 0, 1],
            padded[1, 2, 1],
            padded[1, 1, 0],
            padded[1, 1, 2],
        ],
        axis=0,
    )
    sender_rows = jnp.take(extended, senders.reshape(-1), axis=0)
    degree = senders.size // count
    receiver_part = jnp.dot(node_latents, w_edge_in[:width], preferred_element_type=jnp.float32)
    sender_part = jnp.dot(sender_rows, w_edge_in[width:], preferred_element_type=jnp.float32)
    edge_hidden = jax.nn.silu(
        sender_part.reshape(count, degree, width) + receiver_part[:, None, :]
    ).astype(jnp.bfloat16)
    messages = jnp.dot(
        edge_hidden.reshape(count * degree, width), w_edge_out, preferred_element_type=jnp.float32
    )
    aggregated = jnp.sum(messages.reshape(count, degree, width), axis=1).astype(jnp.bfloat16)
    clusters_here = cluster_latents.shape[0]
    one_hot = (membership[:, None] == jnp.arange(clusters_here, dtype=jnp.int32)[None, :]).astype(
        jnp.bfloat16
    )
    own_cluster = jnp.dot(one_hot, cluster_latents, preferred_element_type=jnp.float32).astype(
        jnp.bfloat16
    )
    preact = jnp.dot(node_latents, w_node_in[:width], preferred_element_type=jnp.float32)
    preact = preact + jnp.dot(
        aggregated, w_node_in[width : 2 * width], preferred_element_type=jnp.float32
    )
    preact = preact + jnp.dot(
        attended, w_node_in[2 * width : 3 * width], preferred_element_type=jnp.float32
    )
    preact = preact + jnp.dot(
        own_cluster, w_node_in[3 * width :], preferred_element_type=jnp.float32
    )
    node_hidden = jax.nn.silu(preact).astype(jnp.bfloat16)
    update = jnp.dot(node_hidden, w_node_out, preferred_element_type=jnp.float32)
    centred = update - jnp.mean(update, axis=1, keepdims=True)
    variance = jnp.mean(centred * centred, axis=1, keepdims=True)
    normed = centred * lax.rsqrt(variance + 1e-05)
    return (node_latents.astype(jnp.float32) + normed * out_gain).astype(jnp.bfloat16)


def solution(mesh):
    in_specs = (
        P(("gx", "gy", "gz"), None),
        P(("gx", "gy", "gz"), None),
        P(("gx", "gy", "gz"), None),
        P(("gx", "gy", "gz")),
        P(),
        P(),
        P(),
        P(),
        P(),
        P(),
        P(),
    )
    out_specs = P(("gx", "gy", "gz"), None)
    return jax.shard_map(
        on_device, mesh=mesh, in_specs=in_specs, out_specs=out_specs, check_vma=False
    )
```

profile of v0, /device:TPU:2, one launch (start us, length us, event | category | flops | bytes accessed | tf_op | source)
XLA Modules:
  0.0 96.1 jit_solution(10848484753565374060)
XLA Ops:
  6.5 0.0 all-gather.2.cloned.1.call-start
  6.6 1.6 %slice_bitcast_fusion = bf16[1,1,1,512,128]{4,3,2,1,0:T(8,128)(2,1)} fusion(bf16[1024,128]{1,0:T(8,128)(2,1)} %param.11), kind=kLoop, calls=%fused_computation.61 | loop fusion | bytes 262144 | tf_op jit(solution)/shard_map/reshape | solution.py:123
  8.2 1.6 %collective-permute-start = (bf16[1,1,1,512,128]{4,3,2,1,0:T(8,128)(2,1)}, bf16[1,1,1,512,128]{4,3,2,1,0:T(8,128)(2,1)}, u32[]{:S(2)}, u32[]{:S(2)}) collective-permute-start(bf16[1,1,1,512,128]{4,3,2,1,0:T(8,128)(2,1)} %slice_bitcast_fusion), channel_id=1, source_target_pairs={{0,32},{32,64},{64,96},{96,128},{128,160},{160,192},{192,224},{224... | collective-permute-start | bytes 393224 | tf_op jit(solution)/shard_map/ppermute | solution.py:56
  9.8 4.1 %collective-permute-start.1 = (bf16[1,1,1,512,128]{4,3,2,1,0:T(8,128)(2,1)}, bf16[1,1,1,512,128]{4,3,2,1,0:T(8,128)(2,1)}, u32[]{:S(2)}, u32[]{:S(2)}) collective-permute-start(bf16[1,1,1,512,128]{4,3,2,1,0:T(8,128)(2,1)} %slice_bitcast_fusion), channel_id=1, source_target_pairs={{32,0},{64,32},{96,64},{128,96},{160,128},{192,160},{224,192},{0,2... | collective-permute-start | bytes 393224 | tf_op jit(solution)/shard_map/ppermute | solution.py:57
  13.8 1.7 %collective-permute-start.3 = (bf16[1,1,1,512,128]{4,3,2,1,0:T(8,128)(2,1)}, bf16[1,1,1,512,128]{4,3,2,1,0:T(8,128)(2,1)}, u32[]{:S(2)}, u32[]{:S(2)}) collective-permute-start(bf16[1,1,1,512,128]{4,3,2,1,0:T(8,128)(2,1)} %slice_bitcast_fusion), channel_id=1, source_target_pairs={{8,0},{16,8},{24,16},{0,24},{9,1},{17,9},{25,17},{1,25},{10,2},{18... | collective-permute-start | bytes 393224 | tf_op jit(solution)/shard_map/ppermute | solution.py:57
  15.6 1.9 %collective-permute-start.4 = (bf16[1,1,1,512,128]{4,3,2,1,0:T(8,128)(2,1)}, bf16[1,1,1,512,128]{4,3,2,1,0:T(8,128)(2,1)}, u32[]{:S(2)}, u32[]{:S(2)}) collective-permute-start(bf16[1,1,1,512,128]{4,3,2,1,0:T(8,128)(2,1)} %slice_bitcast_fusion), channel_id=1, source_target_pairs={{0,1},{1,2},{2,3},{3,4},{4,5},{5,6},{6,7},{7,0},{8,9},{9,10},{10,1... | collective-permute-start | bytes 393224 | tf_op jit(solution)/shard_map/ppermute | solution.py:56
  17.5 1.0 %convolution_convert_fusion.1 = bf16[256,128]{0,1:T(8,128)(2,1)S(1)} fusion(bf16[256,128]{1,0:T(8,128)(2,1)S(1)} %copy-done, bf16[128,128]{1,0:T(8,128)(2,1)} %param.16), kind=kOutput, calls=%fused_computation.28 | convolution fusion | flops 8421376 | bytes 163840 | tf_op jit(solution)/shard_map/dot_general | solution.py:69
  18.5 1.0 %convolution_convert_fusion.2 = bf16[256,128]{0,1:T(8,128)(2,1)S(1)} fusion(bf16[256,128]{1,0:T(8,128)(2,1)S(1)} %copy-done, bf16[128,128]{1,0:T(8,128)(2,1)} %param.15), kind=kOutput, calls=%fused_computation.29 | convolution fusion | flops 8421376 | bytes 163840 | tf_op jit(solution)/shard_map/dot_general | solution.py:69
  19.5 0.7 pad_maximum_fusion
  20.1 0.0 all-gather.2.cloned.1.call-update
  20.1 1.0 %copy.16 = bf16[256,256]{1,0:T(8,128)(2,1)S(1)} copy(bf16[256,256]{0,1:T(8,128)(2,1)} %pad_maximum_fusion) | data formatting | bytes 262144 | tf_op jit(solution)/shard_map/concatenate | solution.py:35
  21.2 1.1 %broadcast_in_dim.13 = bf16[8,256,256]{2,1,0:T(8,128)(2,1)} broadcast(bf16[256,256]{1,0:T(8,128)(2,1)S(1)} %copy.16), dimensions={1,2} | broadcast | bytes 1179648 | tf_op jit(solution)/shard_map/broadcast_in_dim | solution.py:15
  22.2 3.6 %all-to-all-start = ((bf16[8,256,256]{2,1,0:T(8,128)(2,1)}), bf16[8,256,256]{2,1,0:T(8,128)(2,1)S(1)}, u32[]{:S(2)}, u32[]{:S(2)}) async-start(bf16[8,256,256]{2,1,0:T(8,128)(2,1)} %broadcast_in_dim.13), calls=%async_computation | async-start | bytes 2097152 | tf_op jit(solution)/shard_map/all_to_all | solution.py:14
  25.8 16.2 %all_gather.6 = bf16[1024,256]{0,1:T(8,128)(2,1)S(1)} all-gather(bf16[256,256]{0,1:T(8,128)(2,1)} %pad_maximum_fusion), channel_id=1, replica_groups=mesh['gx'=8,'gy'=4,'gz'=8] {'gy'}, dimensions={0}, use_global_device_ids=true | all-gather | bytes 655360 | tf_op jit(solution)/shard_map/all_gather | solution.py:45
  42.0 1.9 %multiply_reduce_fusion.2 = (f32[1024]{0:T(1024)S(1)}, f32[1024,1024]{1,0:T(8,128)S(1)}) fusion(bf16[1024,128]{1,0:T(8,128)(2,1)} %param.11, bf16[1024,256]{0,1:T(8,128)(2,1)S(1)} %all_gather.6), kind=kOutput, calls=%fused_computation.13 | convolution fusion | flops 270531584 | bytes 4722688 | tf_op jit(solution)/shard_map/dot_general | solution.py:74
  44.0 0.2 fusion.50
  44.2 1.0 %fusion.53 = f32[1024,128]{1,0:T(8,128)S(1)} fusion(bf16[1024,128]{1,0:T(8,128)(2,1)S(1)} %copy-done.3, bf16[512,128]{1,0:T(8,128)(2,1)} %param.19), kind=kOutput, calls=%fused_computation.71 | convolution fusion | flops 33554432 | bytes 819200 | tf_op jit(solution)/shard_map/dot_general | solution.py:155
  45.2 0.6 copy-done.1
  45.9 1.3 %fusion.8 = f32[1024]{0:T(1024)} fusion(f32[1024,1024]{1,0:T(8,128)S(1)} %get-tuple-element.10, f32[1024]{0:T(1024)S(1)} %broadcast_maximum_fusion.1), kind=kLoop, calls=%fused_computation.14 | loop fusion | flops 3144704 | bytes 4202496 | tf_op jit(solution)/shard_map/reduce_sum | solution.py:80
  47.2 0.6 compare_and_fusion
  47.8 0.8 copy.15
  48.7 4.3 %collective-permute-start.5 = (bf16[1,1,1,512,128]{4,3,2,1,0:T(8,128)(2,1)}, bf16[1,1,1,512,128]{4,3,2,1,0:T(8,128)(2,1)S(1)}, u32[]{:S(2)}, u32[]{:S(2)}) collective-permute-start(bf16[1,1,1,512,128]{4,3,2,1,0:T(8,128)(2,1)} %slice_bitcast_fusion), channel_id=1, source_target_pairs={{1,0},{2,1},{3,2},{4,3},{5,4},{6,5},{7,6},{0,7},{9,8},{10,9},{11,1... | collective-permute-start | bytes 393224 | tf_op jit(solution)/shard_map/ppermute | solution.py:57
  53.0 0.9 bitcast_dynamic-update-slice_fusion.5
  53.9 0.9 bitcast_dynamic-update-slice_fusion.4
  54.8 0.9 bitcast_dynamic-update-slice_fusion.3
  55.8 0.9 bitcast_dynamic-update-slice_fusion.2
  56.7 0.9 bitcast_dynamic-update-slice_fusion.1
  57.7 15.2 %gather_fusion = bf16[4096,128]{1,0:T(8,128)(2,1)} fusion(bf16[4096,128]{1,0:T(8,128)(2,1)S(1)} %bitcast_dynamic-update-slice_fusion, s32[4096]{0:T(1024)S(1)} %broadcast_clamp_fusion), kind=kCustom, calls=%fused_computation | custom fusion | bytes 2113536 | tf_op jit(solution)/shard_map/jit(_take)/gather | solution.py:137
  72.9 0.4 add.85
  73.2 2.1 %multiply_convert_fusion = bf16[4096,128]{1,0:T(8,128)(2,1)S(1)} fusion(f32[4096,128]{1,0:T(8,128)S(1)} %bitcast.41, bf16[4096,128]{1,0:T(8,128)(2,1)} %gather_fusion, pred[4096]{0:T(1024)(128)(4,1)} %compare_and_fusion, bf16[256,128]{1,0:T(8,128)(2,1)S(1)} %copy-done.11), kind=kOutput, calls=%fused_computation.19 | convolution fusion | flops 137887744 | bytes 4231168 | tf_op jit(solution)/shard_map/dot_general | solution.py:140
  75.4 0.4 convolution_reduce_fusion
  75.8 0.2 convolution_add_fusion.3
  76.0 1.3 %multiply_reduce_fusion.1 = (f32[1024]{0:T(1024)S(1)}, f32[2048,1024]{1,0:T(8,128)S(1)}) fusion(bf16[1024,128]{1,0:T(8,128)(2,1)S(1)} %copy-done.3, bf16[2048,256]{1,0:T(8,128)(2,1)S(1)} %bitcast.39), kind=kOutput, calls=%fused_computation.4 | convolution fusion | flops 541064192 | bytes 9179136 | tf_op jit(solution)/shard_map/dot_general | solution.py:74
  77.3 1.4 %fusion = f32[1024]{0:T(1024)S(1)} fusion(f32[2048,1024]{1,0:T(8,128)S(1)} %get-tuple-element.8, f32[1024]{0:T(1024)S(1)} %broadcast_maximum_fusion.2), kind=kLoop, calls=%fused_computation.5 | loop fusion | flops 6290432 | bytes 8396800 | tf_op jit(solution)/shard_map/reduce_sum | solution.py:80
  78.7 1.6 %fusion.26 = f32[1024,128]{0,1:T(8,128)S(1)} fusion(f32[2048,1024]{1,0:T(8,128)S(1)} %get-tuple-element.8, f32[1024]{0:T(1024)S(1)} %broadcast_maximum_fusion.2, bf16[2048,256]{1,0:T(8,128)(2,1)S(1)} %bitcast.40, f32[1024]{0:T(1024)S(1)} %fusion), kind=kOutput, calls=%fused_computation.34 | convolution fusion | flops 543293440 | bytes 9445376 | tf_op jit(solution)/shard_map/dot_general | solution.py:81
  80.4 0.0 all-gather.2.cloned.1.call-done
  80.4 2.4 %multiply_reduce_fusion = (f32[1024]{0:T(1024)S(1)}, f32[2048,1024]{1,0:T(8,128)S(1)}) fusion(bf16[1024,128]{1,0:T(8,128)(2,1)S(1)} %copy-done.3, bf16[2048,256]{0,1:T(8,128)(2,1)} %all-gather.2.cloned.1.call-done), kind=kOutput, calls=%fused_computation.3 | convolution fusion | flops 541064192 | bytes 9179136 | tf_op jit(solution)/shard_map/dot_general | solution.py:74
  82.9 1.4 %fusion.2 = f32[1024]{0:T(1024)S(1)} fusion(f32[2048,1024]{1,0:T(8,128)S(1)} %get-tuple-element.6, f32[1024]{0:T(1024)S(1)} %broadcast_maximum_fusion), kind=kLoop, calls=%fused_computation.7 | loop fusion | flops 6290432 | bytes 8396800 | tf_op jit(solution)/shard_map/reduce_sum | solution.py:80
  84.3 0.0 copy-start.17
  84.3 0.0 copy-start.10
  84.4 1.6 %fusion.29 = f32[1024,128]{0,1:T(8,128)S(1)} fusion(f32[2048,1024]{1,0:T(8,128)S(1)} %get-tuple-element.6, f32[1024]{0:T(1024)S(1)} %broadcast_maximum_fusion, bf16[2048,256]{0,1:T(8,128)(2,1)S(1)} %copy-done.7, f32[1024]{0:T(1024)S(1)} %fusion.2), kind=kOutput, calls=%fused_computation.35 | convolution fusion | flops 543293440 | bytes 9445376 | tf_op jit(solution)/shard_map/dot_general | solution.py:81
  86.1 0.9 multiply_reduce_fusion.4
  87.0 0.3 convolution_add_fusion.2
  87.3 0.6 multiply_convert_fusion.1
  87.9 0.3 fusion.59
  88.2 0.1 multiply_reduce_fusion.3
  88.3 0.1 add_convert_fusion
  88.5 0.8 copy.17
  (51 shorter events, 0.2 us)
Async XLA Ops:
  6.5 11.0 %copy-start = (bf16[256,128]{1,0:T(8,128)(2,1)S(1)}, bf16[256,128]{1,0:T(8,128)(2,1)}, u32[]{:S(2)}) copy-start(bf16[256,128]{1,0:T(8,128)(2,1)} %param.12) | copy-start | bytes 196612
  6.5 37.5 %copy-start.3 = (bf16[1024,128]{1,0:T(8,128)(2,1)S(1)}, bf16[1024,128]{1,0:T(8,128)(2,1)}, u32[]{:S(2)}) copy-start(bf16[1024,128]{1,0:T(8,128)(2,1)} %param.11) | copy-start | bytes 786436
  6.5 37.4 %copy-start.9 = (s32[32,128]{1,0:T(8,128)S(1)}, s32[32,128]{1,0:T(8,128)}, u32[]{:S(2)}) copy-start(s32[32,128]{1,0:T(8,128)} %param.13) | copy-start | bytes 49156
  6.5 37.5 %copy-start.11 = (bf16[256,128]{1,0:T(8,128)(2,1)S(1)}, bf16[256,128]{1,0:T(8,128)(2,1)}, u32[]{:S(2)}) copy-start(bf16[256,128]{1,0:T(8,128)(2,1)} %param.17) | copy-start | bytes 196612
  6.5 73.9 %all-gather.2.cloned.1.call-start = ((), (), s32[]{:S(2)}) async-start(), calls=%async_computation.1 | async-start | bytes 1179648 | tf_op jit(solution)/shard_map/all_gather | solution.py:45
  8.2 40.5 %collective-permute-start = (bf16[1,1,1,512,128]{4,3,2,1,0:T(8,128)(2,1)}, bf16[1,1,1,512,128]{4,3,2,1,0:T(8,128)(2,1)}, u32[]{:S(2)}, u32[]{:S(2)}) collective-permute-start(bf16[1,1,1,512,128]{4,3,2,1,0:T(8,128)(2,1)} %slice_bitcast_fusion), channel_id=1, source_target_pairs={{0,32},{32,64},{64,96},{96,128},{128,160},{160,192},{192,224},{224... | collective-permute-start | bytes 393224 | tf_op jit(solution)/shard_map/ppermute | solution.py:56
  9.8 44.1 %collective-permute-start.1 = (bf16[1,1,1,512,128]{4,3,2,1,0:T(8,128)(2,1)}, bf16[1,1,1,512,128]{4,3,2,1,0:T(8,128)(2,1)}, u32[]{:S(2)}, u32[]{:S(2)}) collective-permute-start(bf16[1,1,1,512,128]{4,3,2,1,0:T(8,128)(2,1)} %slice_bitcast_fusion), channel_id=1, source_target_pairs={{32,0},{64,32},{96,64},{128,96},{160,128},{192,160},{224,192},{0,2... | collective-permute-start | bytes 393224 | tf_op jit(solution)/shard_map/ppermute | solution.py:57
  13.8 41.0 %collective-permute-start.2 = (bf16[1,1,1,512,128]{4,3,2,1,0:T(8,128)(2,1)}, bf16[1,1,1,512,128]{4,3,2,1,0:T(8,128)(2,1)}, u32[]{:S(2)}, u32[]{:S(2)}) collective-permute-start(bf16[1,1,1,512,128]{4,3,2,1,0:T(8,128)(2,1)} %slice_bitcast_fusion), channel_id=1, source_target_pairs={{0,8},{8,16},{16,24},{24,0},{1,9},{9,17},{17,25},{25,1},{2,10},{10... | collective-permute-start | bytes 393224 | tf_op jit(solution)/shard_map/ppermute | solution.py:56
  13.8 41.9 %collective-permute-start.3 = (bf16[1,1,1,512,128]{4,3,2,1,0:T(8,128)(2,1)}, bf16[1,1,1,512,128]{4,3,2,1,0:T(8,128)(2,1)}, u32[]{:S(2)}, u32[]{:S(2)}) collective-permute-start(bf16[1,1,1,512,128]{4,3,2,1,0:T(8,128)(2,1)} %slice_bitcast_fusion), channel_id=1, source_target_pairs={{8,0},{16,8},{24,16},{0,24},{9,1},{17,9},{25,17},{1,25},{10,2},{18... | collective-permute-start | bytes 393224 | tf_op jit(solution)/shard_map/ppermute | solution.py:57
  15.6 41.1 %collective-permute-start.4 = (bf16[1,1,1,512,128]{4,3,2,1,0:T(8,128)(2,1)}, bf16[1,1,1,512,128]{4,3,2,1,0:T(8,128)(2,1)}, u32[]{:S(2)}, u32[]{:S(2)}) collective-permute-start(bf16[1,1,1,512,128]{4,3,2,1,0:T(8,128)(2,1)} %slice_bitcast_fusion), channel_id=1, source_target_pairs={{0,1},{1,2},{2,3},{3,4},{4,5},{5,6},{6,7},{7,0},{8,9},{9,10},{10,1... | collective-permute-start | bytes 393224 | tf_op jit(solution)/shard_map/ppermute | solution.py:56
  22.2 53.8 %all-to-all-start = ((bf16[8,256,256]{2,1,0:T(8,128)(2,1)}), bf16[8,256,256]{2,1,0:T(8,128)(2,1)S(1)}, u32[]{:S(2)}, u32[]{:S(2)}) async-start(bf16[8,256,256]{2,1,0:T(8,128)(2,1)} %broadcast_in_dim.13), calls=%async_computation | async-start | bytes 2097152 | tf_op jit(solution)/shard_map/all_to_all | solution.py:14
  42.0 5.7 %copy-start.4 = (bf16[1024,256]{0,1:T(8,128)(2,1)}, bf16[1024,256]{0,1:T(8,128)(2,1)S(1)}, u32[]{:S(2)}) copy-start(bf16[1024,256]{0,1:T(8,128)(2,1)S(1)} %all_gather.6) | copy-start | bytes 1572868
  43.9 1.9 %copy-start.1 = (f32[1024,1024]{1,0:T(8,128)}, f32[1024,1024]{1,0:T(8,128)S(1)}, u32[]{:S(2)}) copy-start(f32[1024,1024]{1,0:T(8,128)S(1)} %get-tuple-element.10) | copy-start | bytes 12582916
  43.9 3.8 %copy-start.12 = (f32[1024]{0:T(1024)}, f32[1024]{0:T(1024)S(1)}, u32[]{:S(2)}) copy-start(f32[1024]{0:T(1024)S(1)} %broadcast_maximum_fusion.1) | copy-start | bytes 12292
  48.7 9.0 %collective-permute-start.5 = (bf16[1,1,1,512,128]{4,3,2,1,0:T(8,128)(2,1)}, bf16[1,1,1,512,128]{4,3,2,1,0:T(8,128)(2,1)S(1)}, u32[]{:S(2)}, u32[]{:S(2)}) collective-permute-start(bf16[1,1,1,512,128]{4,3,2,1,0:T(8,128)(2,1)} %slice_bitcast_fusion), channel_id=1, source_target_pairs={{1,0},{2,1},{3,2},{4,3},{5,4},{6,5},{7,6},{0,7},{9,8},{10,9},{11,1... | collective-permute-start | bytes 393224 | tf_op jit(solution)/shard_map/ppermute | solution.py:57
  72.9 2.5 %copy-start.16 = (bf16[128,128]{1,0:T(8,128)(2,1)S(1)}, bf16[128,128]{1,0:T(8,128)(2,1)}, u32[]{:S(2)}) copy-start(bf16[128,128]{1,0:T(8,128)(2,1)} %param.18) | copy-start | bytes 98308
  72.9 2.9 %copy-start.8 = (bf16[512,128]{1,0:T(8,128)(2,1)S(1)}, bf16[512,128]{1,0:T(8,128)(2,1)}, u32[]{:S(2)}) copy-start(bf16[512,128]{1,0:T(8,128)(2,1)} %param.19) | copy-start | bytes 393220
  80.4 3.9 %copy-start.7 = (bf16[2048,256]{0,1:T(8,128)(2,1)S(1)}, bf16[2048,256]{0,1:T(8,128)(2,1)}, u32[]{:S(2)}) copy-start(bf16[2048,256]{0,1:T(8,128)(2,1)} %all-gather.2.cloned.1.call-done) | copy-start | bytes 3145732
  82.9 3.2 %copy-start.2 = (f32[1024,1024]{1,0:T(8,128)S(1)}, f32[1024,1024]{1,0:T(8,128)}, u32[]{:S(2)}) copy-start(f32[1024,1024]{1,0:T(8,128)} %copy-done.1) | copy-start | bytes 12582916
  82.9 3.2 %copy-start.5 = (bf16[1024,256]{0,1:T(8,128)(2,1)S(1)}, bf16[1024,256]{0,1:T(8,128)(2,1)}, u32[]{:S(2)}) copy-start(bf16[1024,256]{0,1:T(8,128)(2,1)} %copy-done.4) | copy-start | bytes 1572868
  82.9 3.2 %copy-start.13 = (f32[1024]{0:T(1024)S(1)}, f32[1024]{0:T(1024)}, u32[]{:S(2)}) copy-start(f32[1024]{0:T(1024)} %copy-done.12) | copy-start | bytes 12292
  82.9 3.2 %copy-start.14 = (f32[1024]{0:T(1024)S(1)}, f32[1024]{0:T(1024)}, u32[]{:S(2)}) copy-start(f32[1024]{0:T(1024)} %fusion.8) | copy-start | bytes 12292
  84.3 3.0 %copy-start.17 = (s32[1024]{0:T(1024)S(1)}, s32[1024]{0:T(1024)}, u32[]{:S(2)}) copy-start(s32[1024]{0:T(1024)} %param.14) | copy-start | bytes 12292
  84.3 3.6 %copy-start.10 = (bf16[128,128]{1,0:T(8,128)(2,1)S(1)}, bf16[128,128]{1,0:T(8,128)(2,1)}, u32[]{:S(2)}) copy-start(bf16[128,128]{1,0:T(8,128)(2,1)} %param.20) | copy-start | bytes 98308
  86.1 2.2 %copy-start.6 = (bf16[1024,128]{0,1:T(8,128)(2,1)S(1)}, bf16[1024,128]{0,1:T(8,128)(2,1)}, u32[]{:S(2)}) copy-start(bf16[1024,128]{0,1:T(8,128)(2,1)} %copy.15) | copy-start | bytes 786436
  86.1 2.2 %copy-start.15 = (f32[128]{0:T(128)S(1)}, f32[128]{0:T(128)}, u32[]{:S(2)}) copy-start(f32[128]{0:T(128)} %param.21) | copy-start | bytes 1540
Sparse Core Ops, SparseCore 0:
  20.3 40.3 all-gather.1
where the time goes:
time: 98 us; the launch traced here: 96.1 us
  local copies, waits for them, and re-layouts  26.3 us (27%)
  starting transfers between devices  17.2 us (18%)
  matrix products  16.7 us (17%)
  blocking collectives  16.2 us (17%)
  between operations  13.9 us (14%)
  other arithmetic  5.71 us (6%)
    all_gather x1, blocking collectives, in_one_piece_2(): lax.all_gather(both, axis, axis=dim, tiled=True)  16.2 us
    gather x1, local copies, waits for them, and re-layouts, on_device(): sender_rows = jnp.take(extended, senders.reshape(-1), axis=0)  15.2 us
    ppermute x3, starting transfers between devices, with_halo(): lax.ppermute(initial, axis, [(b, a) for a, b in up])  10.1 us
    unnamed x43, local copies, waits for them, and re-layouts  6.19 us
    dot_general x3, matrix products, absorb_into(): lax.dot_general(queries, key_rows, (((1,), (1,)), ((), ())), preferred_el...  5.54 us
    dot_general x3, matrix products, absorb_into(): jnp.dot(exponent.astype(jnp.bfloat16), value_rows, preferred_element_type...  4.22 us
    reduce_sum x3, other arithmetic, absorb_into(): running_sum = jnp.sum(exponent, axis=1)  4.19 us
    all_to_all x1, starting transfers between devices, from_everyone(): lax.all_to_all(jnp.broadcast_to(shard[None], (size, *shard.shape)), axis,...  3.56 us
  transfers between devices with their start and end apart: 8, of which 0 were waited for; matrix products, arithmetic and copies ran while one was open for 39% of the time, Pallas kernels for 0%

commit v1 on v0

v1 whole, which is shorter than its diff:
```python
import functools
import math

import jax
import jax.numpy as jnp
from jax import lax
from jax.experimental import pallas as pl
from jax.experimental.pallas import tpu as pltpu
from jax.sharding import PartitionSpec as P

MESH = pl.DeviceIdType.MESH
F32 = jnp.float32
BF16 = jnp.bfloat16
ROWS = 256
NT = (((1,), (1,)), ((), ()))


def dot(a, b):
    return jnp.dot(a, b, preferred_element_type=F32)


def silu(x):
    half = 0.5 * x
    return half * jnp.tanh(half) + half


def kernel(
    nodes_h, clusters_h, senders, members, wk_h, wv_h, wei_h, weo_h, wni_h, wno_h, gain_h,
    out_h,
    nodes, clusters, wk, wv, wei, weo, wni, wno, gain,
    far, faces, table, ctable, planes, keys, values, first, lines, out_v,
    load_sem, send_sem, recv_sem, out_sem,
):
    count, width = nodes.shape
    held = clusters.shape[0]
    bound = faces.shape[1]
    gx, gy, gz = (lax.axis_index(a) for a in ("gx", "gy", "gz"))
    nx, ny, nz = (lax.axis_size(a) for a in ("gx", "gy", "gz"))
    scale = math.log2(math.e) / math.sqrt(width)

    def along(axis, step):
        at, size = {"gx": (gx, nx), "gy": (gy, ny), "gz": (gz, nz)}[axis]
        return {axis: lax.rem(at + (step % size), size)}

    line = [("gy", s) for s in range(1, ny)]
    line += [("gz", s) for s in range(1, nz)] + [("gx", s) for s in range(1, nx)]
    halo = [(axis, step) for axis in ("gx", "gy", "gz") for step in (1, -1)]

    barrier = pltpu.get_barrier_semaphore()
    for axis, step in line:
        pl.semaphore_signal(barrier, inc=1, device_id=along(axis, step), device_id_type=MESH)

    loads = [
        pltpu.make_async_copy(src, dst, load_sem.at[i])
        for i, (src, dst) in enumerate(
            (
                (nodes_h, nodes), (clusters_h, clusters), (wk_h, wk), (wv_h, wv), (wei_h, wei),
                (weo_h, weo), (wni_h, wni), (wno_h, wno), (gain_h, gain),
            )
        )
    ]
    for copy in loads:
        copy.start()
    loads[0].wait()
    loads[1].wait()
    pl.semaphore_wait(barrier, len(line))

    border = nodes.at[pl.ds(0, bound)]
    sends = []
    for i, (axis, step) in enumerate(halo):
        sends.append(
            pltpu.make_async_remote_copy(
                src_ref=border, dst_ref=faces.at[i], send_sem=send_sem.at[i],
                recv_sem=recv_sem.at[i], device_id=along(axis, step), device_id_type=MESH,
            )
        )
    for i, (axis, step) in enumerate(line):
        j = len(halo) + i
        sends.append(
            pltpu.make_async_remote_copy(
                src_ref=clusters, dst_ref=far.at[i], send_sem=send_sem.at[j],
                recv_sem=recv_sem.at[j], device_id=along(axis, step), device_id_type=MESH,
            )
        )
    for copy in sends:
        copy.start()
    for copy in loads[2:]:
        copy.wait()

    w_kv = jnp.concatenate([wk[...], wv[...]], axis=1)
    values[:, pl.ds(width, width)] = jnp.ones((values.shape[0], width), BF16)

    def project(block, at):
        both = dot(block, w_kv)
        rows = pl.ds(at * held, held)
        keys[rows, :] = both[:, :width].astype(BF16)
        values[rows, pl.ds(0, width)] = both[:, width:].astype(BF16)

    def attend(blocks, before, after):
        reach = pl.ds(0, blocks * held)

        def step(i, carry):
            rows = pl.ds(pl.multiple_of(i * ROWS, ROWS), ROWS)
            scores = lax.dot_general(nodes[rows, :], keys[reach, :], NT, preferred_element_type=F32)
            top = jnp.max(scores, axis=1, keepdims=True)
            if before is None:
                top = jnp.broadcast_to(top, (ROWS, width))
            else:
                old = before[rows, pl.ds(0, width)]
                top = jnp.maximum(old, top)
                fade = jnp.exp2((old - top) * scale)
            weights = jnp.concatenate(
                [
                    jnp.exp2((scores[:, g : g + width] - top) * scale).astype(BF16)
                    for g in range(0, blocks * held, width)
                ],
                axis=1,
            )
            gained = dot(weights, values[reach, :])
            if before is not None:
                gained = gained + before[rows, pl.ds(width, 2 * width)] * jnp.concatenate([fade, fade], axis=1)
            after[rows, pl.ds(0, width)] = top
            after[rows, pl.ds(width, 2 * width)] = gained
            return carry

        lax.fori_loop(0, count // ROWS, step, 0)

    w_sender = wei[pl.ds(width, width), :]
    project(clusters[...], 0)
    attend(1, None, first)
    table[pl.ds(0, count), :] = dot(nodes[...], w_sender)
    ctable[...] = dot(clusters[...], wni[pl.ds(3 * width, width), :])

    at = 0
    for which, size in enumerate((ny, nz, nx)):
        state = lines.at[which]
        before = first
        todo = list(range(at, at + size - 1))
        at += size - 1
        while todo:
            part, todo = (todo, []) if len(todo) <= 3 else (todo[:2], todo[2:])
            for k, i in enumerate(part):
                sends[len(halo) + i].wait_recv()
                project(far[i], k)
            attend(len(part), before, state)
            before = state

    for i in range(len(halo)):
        sends[i].wait_recv()
        table[pl.ds(count + i * bound, bound), :] = dot(faces[i], w_sender)

    degree = senders.shape[0] * senders.shape[1] // count
    unroll = 8

    def pick(i, carry):
        base = pl.multiple_of(i * unroll, unroll)
        per = 128 // degree
        for k in range(unroll):
            for j in range(degree):
                flat = (base + k) * degree + j
                e = senders[lax.div(flat, 128), lax.rem(flat, 128)]
                planes[j, pl.ds(base + k, 1), :] = table[pl.ds(e, 1), :]
            planes[degree, pl.ds(base + k, 1), :] = ctable[pl.ds(members[base + k], 1), :]
        return carry

    lax.fori_loop(0, count // unroll, pick, 0)

    w_out = weo[...]
    w_outs = jnp.concatenate([w_out] * degree, axis=0)
    eps_pool, eps_norm = 1e-06, 1e-05

    def finish(i, carry):
        rows = pl.ds(pl.multiple_of(i * ROWS, ROWS), ROWS)
        own = nodes[rows, :]
        receiver = dot(own, wei[pl.ds(0, width), :])
        hidden = jnp.concatenate([silu(planes[j, rows, :] + receiver).astype(BF16) for j in range(degree)], axis=1)
        aggregated = dot(hidden, w_outs).astype(BF16)
        pooled = jnp.zeros((ROWS, width), F32)
        for which in range(3):
            pooled = pooled + lines[which, rows, pl.ds(width, width)] / lines[which, rows, pl.ds(2 * width, width)]
        attended = (pooled * lax.rsqrt(jnp.mean(pooled * pooled, axis=1, keepdims=True) + eps_pool)).astype(BF16)
        mixed = jnp.concatenate([own, aggregated, attended], axis=1)
        preact = dot(mixed, wni[pl.ds(0, 3 * width), :]) + planes[degree, rows, :]
        update = dot(silu(preact).astype(BF16), wno[...])
        centred = update - jnp.mean(update, axis=1, keepdims=True)
        variance = jnp.mean(centred * centred, axis=1, keepdims=True)
        normed = centred * lax.rsqrt(variance + eps_norm)
        out_v[rows, :] = (own.astype(F32) + normed * gain[...]).astype(BF16)
        return carry

    lax.fori_loop(0, count // ROWS, finish, 0)
    copy = pltpu.make_async_copy(out_v, out_h, out_sem)
    copy.start()
    for sent in sends:
        sent.wait_send()
    copy.wait()


def on_device(mesh, *args):
    nodes, clusters, senders, members, wk, wv, wei, weo, wni, wno, gain = args
    count, width = nodes.shape
    held = clusters.shape[0]
    bound = count // 2
    copies = sum(mesh.shape[a] - 1 for a in ("gx", "gy", "gz"))
    degree = senders.size // count
    hbm = pl.BlockSpec(memory_space=pl.ANY)
    smem = pl.BlockSpec(memory_space=pltpu.SMEM)
    vmem = lambda a: pltpu.VMEM(a.shape, a.dtype)
    gain = gain.reshape(1, width)
    return pl.pallas_call(
        kernel,
        out_shape=jax.ShapeDtypeStruct((count, width), BF16),
        in_specs=[hbm, hbm, smem, smem] + [hbm] * 7,
        out_specs=hbm,
        scratch_shapes=[
            *(vmem(a) for a in (nodes, clusters, wk, wv, wei, weo, wni, wno, gain)),
            pltpu.VMEM((copies, held, width), BF16),
            pltpu.VMEM((6, bound, width), BF16),
            pltpu.VMEM((count + 6 * bound, width), F32),
            pltpu.VMEM((held, width), F32),
            pltpu.VMEM((degree + 1, count, width), F32),
            pltpu.VMEM((3 * held, width), BF16),
            pltpu.VMEM((3 * held, 2 * width), BF16),
            pltpu.VMEM((count, 3 * width), F32),
            pltpu.VMEM((3, count, 3 * width), F32),
            pltpu.VMEM((count, width), BF16),
            pltpu.SemaphoreType.DMA((9,)),
            pltpu.SemaphoreType.DMA((6 + copies,)),
            pltpu.SemaphoreType.DMA((6 + copies,)),
            pltpu.SemaphoreType.DMA,
        ],
        compiler_params=pltpu.CompilerParams(collective_id=0, has_side_effects=True),
        name="layer",
    )(nodes, clusters, senders, members, wk, wv, wei, weo, wni, wno, gain)


def solution(mesh):
    blocks = ("gx", "gy", "gz")
    in_specs = (P(blocks, None), P(blocks, None), P(blocks, None), P(blocks)) + (P(),) * 7
    return jax.shard_map(
        functools.partial(on_device, mesh),
        mesh=mesh, in_specs=in_specs, out_specs=P(blocks, None), check_vma=False,
    )
```

time: 98 us -> 69.3 us (0.71); the launches traced: 96.1 us -> 69.1 us
  Pallas kernels: 0 us -> 67.4 us
  local copies, waits for them, and re-layouts: 26.3 us -> 1.67 us
  starting transfers between devices: 17.2 us -> 0 us
  matrix products: 16.7 us -> 0 us
  blocking collectives: 16.2 us -> 0 us
  between operations: 13.9 us -> 0.01 us
  other arithmetic: 5.71 us -> 0 us
    pallas_call x0 -> x1, Pallas kernels: none -> 67.4 us  [on_device(): pl.pallas_call(kernel, out_shape=jax.ShapeDtypeStruct((count, width), BF1...]
    dot_general x16 -> x0, matrix products: 16.7 us -> none  [the longest x3 5.54 us: absorb_into(): lax.dot_general(queries, key_rows, (((1,), (1,)), ((), ())), preferred_el...]
    all_gather x1 -> x0, blocking collectives: 16.2 us -> none  [in_one_piece_2(): lax.all_gather(both, axis, axis=dim, tiled=True)]
    gather x1 -> x0, local copies, waits for them, and re-layouts: 15.2 us -> none  [on_device(): sender_rows = jnp.take(extended, senders.reshape(-1), axis=0)]
    ppermute x6 -> x0, starting transfers between devices: 13.6 us -> none  [the longest x3 10.1 us: with_halo(): lax.ppermute(initial, axis, [(b, a) for a, b in up])]
    unnamed x43 -> x1, local copies, waits for them, and re-layouts: 6.19 us -> 1.67 us
    reduce_sum x4 -> x0, other arithmetic: 4.26 us -> none  [the longest x3 4.19 us: absorb_into(): running_sum = jnp.sum(exponent, axis=1)]
    all_to_all x1 -> x0, starting transfers between devices: 3.56 us -> none  [from_everyone(): lax.all_to_all(jnp.broadcast_to(shard[None], (size, *shard.shape)), axis,...]
  transfers between devices with their start and end apart: 8 -> 0, of which waited for: 0 -> 0; matrix products, arithmetic and copies ran while one was open for 39% -> 0% of each run, Pallas kernels for 0% -> 0%
where the time goes in v1:
time: 69.3 us; the launch traced here: 69.1 us
  Pallas kernels  67.4 us (97%)
  local copies, waits for them, and re-layouts  1.67 us (2%)
    pallas_call x1, Pallas kernels, on_device(): pl.pallas_call(kernel, out_shape=jax.ShapeDtypeStruct((count, width), BF1...  67.4 us
    unnamed x1, local copies, waits for them, and re-layouts  1.67 us

profile of v1, /device:TPU:2, one launch (start us, length us, event | category | flops | bytes accessed | tf_op | source)
XLA Modules:
  0.0 69.1 jit_solution(123252335361015251)
XLA Ops:
  0.0 67.4 %layer.1 = bf16[1024,128]{1,0:T(8,128)(2,1)} custom-call(bf16[1024,128]{1,0:T(8,128)(2,1)} %nodes_h.1, bf16[256,128]{1,0:T(8,128)(2,1)} %clusters_h.1, s32[32,128]{1,0:T(8,128)} %senders.1, s32[1024]{0:T(1024)} %members.1, bf16[128,128]{1,0:T(8,128)(2,1)} %wk_h.1, bf16[128,128]{1,0:T(8,128)(2,1)} %wv_h.1, bf16[256,128]{1,0:T(8,128)(2,1)} %wei_h.1, ...), custom_call_target="tpu_custom_call" | custom-call | tf_op jit(solution)/shard_map/layer/pallas_call | solution.py:210
  67.4 1.7 %copy.13 = bf16[1024,128]{1,0:T(8,128)(2,1)} copy(bf16[1024,128]{1,0:T(8,128)(2,1)} %layer.1) | data formatting | bytes 524288

commit v2 on v1

v2 whole, which is shorter than its diff:
```python
import functools
import math

import jax
import jax.numpy as jnp
from jax import lax
from jax.experimental import pallas as pl
from jax.experimental.pallas import tpu as pltpu
from jax.sharding import PartitionSpec as P

MESH = pl.DeviceIdType.MESH
F32 = jnp.float32
BF16 = jnp.bfloat16
ROWS = 256
BIG = 512
NT = (((1,), (1,)), ((), ()))


def dot(a, b):
    return jnp.dot(a, b, preferred_element_type=F32)


def silu(x):
    half = 0.5 * x
    return half * jnp.tanh(half) + half


def kernel(
    nodes_h, clusters_h, senders_h, members_h, wk_h, wv_h, wei_h, weo_h, wni_h, wno_h, gain_h,
    out_h,
    senders, members, nodes, clusters, wk, wv, wei, weo, wni, wno, gain,
    far, faces, table, ctable, planes, keys, values, first, lines, receiver, base, out_v,
    score_a, score_b, weight_a, weight_b, fade_a, fade_b,
    load_sem, send_sem, recv_sem, out_sem,
):
    count, width = nodes.shape
    held = clusters.shape[0]
    bound = faces.shape[1]
    gx, gy, gz = (lax.axis_index(a) for a in ("gx", "gy", "gz"))
    nx, ny, nz = (lax.axis_size(a) for a in ("gx", "gy", "gz"))
    scale = math.log2(math.e) / math.sqrt(width)

    def along(axis, step):
        at, size = {"gx": (gx, nx), "gy": (gy, ny), "gz": (gz, nz)}[axis]
        return {axis: lax.rem(at + (step % size), size)}

    line = [("gy", s) for s in range(1, ny)]
    line += [("gz", s) for s in (1, nz - 1, 2, nz - 2, 3, nz - 3, 4)]
    line += [("gx", s) for s in (1, nx - 1, 2, nx - 2, 3, nx - 3, 4)]
    halo = [(axis, step) for axis in ("gx", "gy", "gz") for step in (1, -1)]

    barrier = pltpu.get_barrier_semaphore()
    for axis, step in line:
        pl.semaphore_signal(barrier, inc=1, device_id=along(axis, step), device_id_type=MESH)

    loads = [
        pltpu.make_async_copy(src, dst, load_sem.at[i])
        for i, (src, dst) in enumerate(
            (
                (nodes_h, nodes), (clusters_h, clusters), (wk_h, wk), (wv_h, wv), (wei_h, wei),
                (weo_h, weo), (wni_h, wni), (wno_h, wno), (gain_h, gain), (senders_h, senders),
                (members_h, members),
            )
        )
    ]
    for copy in loads:
        copy.start()
    with jax.named_scope("load_wait"):
        loads[0].wait()
        loads[1].wait()
    with jax.named_scope("barrier_wait"):
        pl.semaphore_wait(barrier, len(line))

    border = nodes.at[pl.ds(0, bound)]
    sends = []
    for i, (axis, step) in enumerate(halo):
        sends.append(
            pltpu.make_async_remote_copy(
                src_ref=border, dst_ref=faces.at[i], send_sem=send_sem.at[i],
                recv_sem=recv_sem.at[i], device_id=along(axis, step), device_id_type=MESH,
            )
        )
    for i, (axis, step) in enumerate(line):
        j = len(halo) + i
        sends.append(
            pltpu.make_async_remote_copy(
                src_ref=clusters, dst_ref=far.at[i], send_sem=send_sem.at[j],
                recv_sem=recv_sem.at[j], device_id=along(axis, step), device_id_type=MESH,
            )
        )
    for copy in sends:
        copy.start()
    for copy in loads[2:]:
        copy.wait()

    w_kv = jnp.concatenate([wk[...], wv[...]], axis=1)
    values[:, pl.ds(width, width)] = jnp.ones((values.shape[0], width), BF16)

    def project(block, at):
        both = dot(block, w_kv)
        rows = pl.ds(at * held, held)
        keys[rows, :] = both[:, :width].astype(BF16)
        values[rows, pl.ds(0, width)] = both[:, width:].astype(BF16)

    steps = count // ROWS
    score, weight, fades = (score_a, score_b), (weight_a, weight_b), (fade_a, fade_b)

    def attend(at, blocks, before, after):
        span = blocks * held
        reach, near = pl.ds(at * held, span), pl.ds(0, span)

        def rows_of(i):
            return pl.ds(i * ROWS if isinstance(i, int) else pl.multiple_of(i * ROWS, ROWS), ROWS)

        def scores_of(i, p):
            score[p][:, near] = lax.dot_general(nodes[rows_of(i), :], keys[reach, :], NT, preferred_element_type=F32)

        def weights_of(i, p):
            rows = rows_of(i)
            scores = score[p][:, near]
            top = jnp.max(scores, axis=1, keepdims=True)
            if before is None:
                top = jnp.broadcast_to(top, (ROWS, width))
            else:
                old = before[rows, pl.ds(0, width)]
                top = jnp.maximum(old, top)
                fades[p][...] = jnp.exp2((old - top) * scale)
            after[rows, pl.ds(0, width)] = top
            for g in range(0, span, width):
                weight[p][:, pl.ds(g, width)] = jnp.exp2((scores[:, g : g + width] - top) * scale).astype(BF16)

        def sums_of(i, p):
            rows, both = rows_of(i), pl.ds(width, 2 * width)
            gained = dot(weight[p][:, near], values[reach, :])
            if before is not None:
                fade = fades[p][...]
                gained = gained + before[rows, both] * jnp.concatenate([fade, fade], axis=1)
            after[rows, both] = gained

        scores_of(0, 0)
        scores_of(1, 1)
        weights_of(0, 0)

        def step(j, carry):
            for p in range(2):
                sums_of(2 * j + p, p)
                weights_of(2 * j + p + 1, 1 - p)
                scores_of(2 * j + p + 2, p)
            return carry

        with jax.named_scope(f"attend{blocks}"):
            lax.fori_loop(0, steps // 2 - 1, step, 0)
        sums_of(steps - 2, 0)
        weights_of(steps - 1, 1)
        sums_of(steps - 1, 1)

    own_w, sender_w = pl.ds(0, width), pl.ds(width, width)
    project(clusters[...], 0)
    attend(0, 1, None, first)
    table[pl.ds(0, count), :] = dot(nodes[...], wei[sender_w, :])
    receiver[...] = dot(nodes[...], wei[own_w, :])
    ctable[...] = dot(clusters[...], wni[pl.ds(3 * width, width), :])

    for i in range(len(halo)):
        with jax.named_scope(f"wait_halo{i}"):
            sends[i].wait_recv()
        table[pl.ds(count + i * bound, bound), :] = dot(faces[i], wei[sender_w, :])

    degree = senders.shape[0] * senders.shape[1] // count
    lanes = senders.shape[1]
    part = lanes // degree

    def pick(i, carry):
        start = pl.multiple_of(i * part, part)
        for k in range(part):
            for j in range(degree):
                planes[j, pl.ds(start + k, 1), :] = table[pl.ds(senders[i, k * degree + j], 1), :]
            planes[degree, pl.ds(start + k, 1), :] = ctable[pl.ds(members[start + k], 1), :]
        return carry

    with jax.named_scope("gather"):
        lax.fori_loop(0, senders.shape[0], pick, 0)

    w_out = weo[...]
    w_outs = jnp.concatenate([w_out] * degree, axis=0)

    def edges(i, carry):
        rows = pl.ds(pl.multiple_of(i * BIG, BIG), BIG)
        to = receiver[rows, :]
        hidden = jnp.concatenate([silu(planes[j, rows, :] + to).astype(BF16) for j in range(degree)], axis=1)
        aggregated = dot(hidden, w_outs).astype(BF16)
        mixed = jnp.concatenate([nodes[rows, :], aggregated], axis=1)
        base[rows, :] = dot(mixed, wni[pl.ds(0, 2 * width), :]) + planes[degree, rows, :]
        return carry

    with jax.named_scope("edges"):
        lax.fori_loop(0, count // BIG, edges, 0)

    at = 0
    for which, size in enumerate((ny, nz, nx)):
        state = lines.at[which]
        before = first
        todo = list(range(at, at + size - 1))
        at += size - 1
        while todo:
            now = min(len(todo), 3 if len(todo) != 4 else 4)
            now, todo = todo[:now], todo[now:]
            for i in now:
                with jax.named_scope(f"wait_line{i}"):
                    sends[len(halo) + i].wait_recv()
                project(far[i], i + 1)
            attend(now[0] + 1, len(now), before, state)
            before = state

    eps_pool, eps_norm = 1e-06, 1e-05

    def finish(i, carry):
        rows = pl.ds(pl.multiple_of(i * BIG, BIG), BIG)
        pooled = jnp.zeros((BIG, width), F32)
        for which in range(3):
            pooled = pooled + lines[which, rows, pl.ds(width, width)] / lines[which, rows, pl.ds(2 * width, width)]
        attended = (pooled * lax.rsqrt(jnp.mean(pooled * pooled, axis=1, keepdims=True) + eps_pool)).astype(BF16)
        preact = dot(attended, wni[pl.ds(2 * width, width), :]) + base[rows, :]
        update = dot(silu(preact).astype(BF16), wno[...])
        centred = update - jnp.mean(update, axis=1, keepdims=True)
        variance = jnp.mean(centred * centred, axis=1, keepdims=True)
        normed = centred * lax.rsqrt(variance + eps_norm)
        out_v[rows, :] = (nodes[rows, :].astype(F32) + normed * gain[...]).astype(BF16)
        return carry

    with jax.named_scope("finish"):
        lax.fori_loop(0, count // BIG, finish, 0)
    copy = pltpu.make_async_copy(out_v, out_h, out_sem)
    copy.start()
    with jax.named_scope("end"):
        for sent in sends:
            sent.wait_send()
        copy.wait()


def on_device(mesh, *args):
    nodes, clusters, senders, members, wk, wv, wei, weo, wni, wno, gain = args
    count, width = nodes.shape
    held = clusters.shape[0]
    bound = count // 2
    copies = sum(mesh.shape[a] - 1 for a in ("gx", "gy", "gz"))
    degree = senders.size // count
    hbm = pl.BlockSpec(memory_space=pl.ANY)
    vmem = lambda a: pltpu.VMEM(a.shape, a.dtype)
    gain = gain.reshape(1, width)
    return pl.pallas_call(
        kernel,
        out_shape=jax.ShapeDtypeStruct((count, width), BF16),
        in_specs=[hbm] * 11,
        out_specs=hbm,
        scratch_shapes=[
            pltpu.SMEM(senders.shape, senders.dtype),
            pltpu.SMEM(members.shape, members.dtype),
            *(vmem(a) for a in (nodes, clusters, wk, wv, wei, weo, wni, wno, gain)),
            pltpu.VMEM((copies, held, width), BF16),
            pltpu.VMEM((6, bound, width), BF16),
            pltpu.VMEM((count + 6 * bound, width), F32),
            pltpu.VMEM((held, width), F32),
            pltpu.VMEM((degree + 1, count, width), F32),
            pltpu.VMEM(((copies + 1) * held, width), BF16),
            pltpu.VMEM(((copies + 1) * held, 2 * width), BF16),
            pltpu.VMEM((count, 3 * width), F32),
            pltpu.VMEM((3, count, 3 * width), F32),
            pltpu.VMEM((count, width), F32),
            pltpu.VMEM((count, width), F32),
            pltpu.VMEM((count, width), BF16),
            *[pltpu.VMEM((ROWS, 4 * held), F32)] * 2,
            *[pltpu.VMEM((ROWS, 4 * held), BF16)] * 2,
            *[pltpu.VMEM((ROWS, width), F32)] * 2,
            pltpu.SemaphoreType.DMA((11,)),
            pltpu.SemaphoreType.DMA((6 + copies,)),
            pltpu.SemaphoreType.DMA((6 + copies,)),
            pltpu.SemaphoreType.DMA,
        ],
        compiler_params=pltpu.CompilerParams(collective_id=0, has_side_effects=True),
        name="layer",
    )(nodes, clusters, senders, members, wk, wv, wei, weo, wni, wno, gain)


def solution(mesh):
    blocks = ("gx", "gy", "gz")
    in_specs = (P(blocks, None), P(blocks, None), P(blocks, None), P(blocks)) + (P(),) * 7
    return jax.shard_map(
        functools.partial(on_device, mesh),
        mesh=mesh, in_specs=in_specs, out_specs=P(blocks, None), check_vma=False,
    )
```

time: 69.3 us -> 37.4 us (0.54)
  Pallas kernels: 67.4 us -> 35.5 us
    pallas_call x1, Pallas kernels: 67.4 us -> 35.5 us  [on_device(): pl.pallas_call(kernel, out_shape=jax.ShapeDtypeStruct((count, width), BF1...]
where the time goes in v2:
time: 37.4 us; the launch traced here: 37.2 us
  Pallas kernels  35.5 us (95%)
  local copies, waits for them, and re-layouts  1.67 us (4%)
    pallas_call x1, Pallas kernels, on_device(): pl.pallas_call(kernel, out_shape=jax.ShapeDtypeStruct((count, width), BF1...  35.5 us
    unnamed x1, local copies, waits for them, and re-layouts  1.67 us

profile of v2, /device:TPU:2, one launch (start us, length us, event | category | flops | bytes accessed | tf_op | source)
XLA Modules:
  0.0 37.2 jit_solution(3981082094353640816)
XLA Ops:
  0.0 35.5 %layer.1 = bf16[1024,128]{1,0:T(8,128)(2,1)} custom-call(bf16[1024,128]{1,0:T(8,128)(2,1)} %nodes_h.1, bf16[256,128]{1,0:T(8,128)(2,1)} %clusters_h.1, s32[32,128]{1,0:T(8,128)} %senders_h.1, s32[1024]{0:T(1024)} %members_h.1, bf16[128,128]{1,0:T(8,128)(2,1)} %wk_h.1, bf16[128,128]{1,0:T(8,128)(2,1)} %wv_h.1, bf16[256,128]{1,0:T(8,128)(2,1)} %wei_h.1, ...), custom_call_target="tpu_custom_call" | custom-call | tf_op jit(solution)/shard_map/layer/pallas_call | solution.py:251
  35.5 1.7 %copy.13 = bf16[1024,128]{1,0:T(8,128)(2,1)} copy(bf16[1024,128]{1,0:T(8,128)(2,1)} %layer.1) | data formatting | bytes 524288

commit v3 on v2

v3 whole, which is shorter than its diff:
```python
import functools
import math

import jax
import jax.numpy as jnp
from jax import lax
from jax.experimental import pallas as pl
from jax.experimental.pallas import tpu as pltpu
from jax.sharding import PartitionSpec as P

MESH = pl.DeviceIdType.MESH
F32 = jnp.float32
BF16 = jnp.bfloat16
ROWS = 256
BIG = 512
NT = (((1,), (1,)), ((), ()))


def dot(a, b):
    return jnp.dot(a, b, preferred_element_type=F32)


def silu(x):
    half = 0.5 * x
    return half * jnp.tanh(half) + half


def kernel(
    nodes_h, clusters_h, senders_h, members_h, wk_h, wv_h, wei_h, weo_h, wni_h, wno_h, gain_h,
    out_h,
    senders, members, nodes, clusters, wk, wv, wei, weo, wni, wno, gain,
    far, faces, table, ctable, planes, keys, values, first, lines, receiver, base, out_v,
    score_a, score_b, weight_a, weight_b, fade_a, fade_b,
    load_sem, send_sem, recv_sem, out_sem,
):
    count, width = nodes.shape
    held = clusters.shape[0]
    bound = faces.shape[0] // 6
    gx, gy, gz = (lax.axis_index(a) for a in ("gx", "gy", "gz"))
    nx, ny, nz = (lax.axis_size(a) for a in ("gx", "gy", "gz"))
    scale = math.log2(math.e) / math.sqrt(width)

    half = ny_ring = nx // 2
    upper, ring = lax.div(gx, ny_ring), lax.rem(gx, ny_ring)

    def to_gy(d):
        return {"gy": lax.rem(gy + d % ny, ny)}

    def to_gz(d):
        return {"gz": lax.rem(gz + d % nz, nz)}

    def to_gx(d):
        return {"gx": lax.rem(gx + d % nx, nx)}

    def to_ring(d):
        return {"gx": upper * ny_ring + lax.rem(ring + d % ny_ring, ny_ring)}

    across = {"gx": lax.rem(gx + half, nx)}
    halo = [to_gx(1), to_gx(-1), to_gy(1), to_gy(-1), to_gz(1), to_gz(-1)]
    partners = [to_gy(d) for d in (1, 2, 3)] + [to_gz(d) for d in (1, -1, 2, -2)]
    partners += [across] + [to_ring(d) for d in (1, -1, 2)] + [to_gx(1), to_gx(-1)]

    barrier = pltpu.get_barrier_semaphore()
    for device in partners:
        pl.semaphore_signal(barrier, inc=1, device_id=device, device_id_type=MESH)

    loads = [
        pltpu.make_async_copy(src, dst, load_sem.at[i])
        for i, (src, dst) in enumerate(
            (
                (nodes_h, nodes), (clusters_h, clusters), (wk_h, wk), (wv_h, wv), (wei_h, wei),
                (weo_h, weo), (wni_h, wni), (wno_h, wno), (gain_h, gain), (senders_h, senders),
                (members_h, members),
            )
        )
    ]
    for copy in loads:
        copy.start()
    with jax.named_scope("load_wait"):
        loads[0].wait()
        loads[1].wait()
    with jax.named_scope("barrier_wait"):
        pl.semaphore_wait(barrier, len(partners))

    slots = ["y1", "y2", "y3", "z-1", "z1", "z-2", "z2", "z-3", "z3", "z4"]
    slots += ["x", "r-1", "r1", "r2", "xr-1", "xr1", "xr2"]
    slot = {name: i for i, name in enumerate(slots)}
    copies = {}

    def send(key, src, dst, device):
        i = len(copies)
        copies[key] = pltpu.make_async_remote_copy(
            src_ref=src, dst_ref=dst, send_sem=send_sem.at[i], recv_sem=recv_sem.at[i],
            device_id=device, device_id_type=MESH,
        )
        copies[key].start()

    def cell(name, start=0, size=held):
        return far.at[pl.ds(slot[name] * held + start, size)]

    send("x", clusters, cell("x"), across)
    send("z-2", clusters, cell("z-2"), to_gz(2))
    send("z2", clusters, cell("z2"), to_gz(-2))
    for d in (1, 2, 3):
        send(f"y{d}", clusters, cell(f"y{d}"), to_gy(-d))
    send("z-1", clusters, cell("z-1"), to_gz(1))
    send("z1", clusters, cell("z1"), to_gz(-1))
    send("r-1", clusters, cell("r-1"), to_ring(1))
    send("r1", clusters, cell("r1"), to_ring(-1))
    border = nodes.at[pl.ds(0, bound)]
    for i, device in enumerate(halo):
        send(f"h{i}", border, faces.at[pl.ds(i * bound, bound)], device)
    send("r2", clusters, cell("r2"), to_ring(2))

    def arrive(*names):
        for name in names:
            with jax.named_scope("wait_" + name):
                copies[name].wait_recv()

    def relay_x():
        arrive("x")
        for d in (1, -1, 2):
            name = "xr2" if d == 2 else f"xr{-d}"
            send(name, cell("x"), cell(name), to_ring(d))

    def relay_z():
        for sign, start in ((-1, 0), (1, held // 2)):
            here = f"z{2 * sign}"
            arrive(here)
            send(f"z{3 * sign}", cell(here), cell(f"z{3 * sign}"), to_gz(-sign))
            send(f"z4_{start}", cell(here, start, held // 2), cell("z4", start, held // 2), to_gz(-2 * sign))

    for copy in loads[2:]:
        copy.wait()

    w_kv = jnp.concatenate([wk[...], wv[...]], axis=1)
    values[:, pl.ds(width, width)] = jnp.ones((values.shape[0], width), BF16)

    def project(block, at, blocks):
        both = dot(block, w_kv)
        rows = pl.ds(at * held, blocks * held)
        keys[rows, :] = both[:, :width].astype(BF16)
        values[rows, pl.ds(0, width)] = both[:, width:].astype(BF16)

    steps = count // ROWS
    score, weight, fades = (score_a, score_b), (weight_a, weight_b), (fade_a, fade_b)

    def rows_of(i):
        return pl.ds(i * ROWS, ROWS)

    def scores_of(at, blocks, before, after, i, p):
        reach, near = pl.ds(at * held, blocks * held), pl.ds(0, blocks * held)
        score[p][:, near] = lax.dot_general(nodes[rows_of(i), :], keys[reach, :], NT, preferred_element_type=F32)

    def weights_of(at, blocks, before, after, i, p):
        span = blocks * held
        rows = rows_of(i)
        scores = score[p][:, pl.ds(0, span)]
        top = jnp.max(scores, axis=1, keepdims=True)
        if before is None:
            top = jnp.broadcast_to(top, (ROWS, width))
        else:
            old = before[rows, pl.ds(0, width)]
            top = jnp.maximum(old, top)
            fades[p][...] = jnp.exp2((old - top) * scale)
        after[rows, pl.ds(0, width)] = top
        for g in range(0, span, width):
            weight[p][:, pl.ds(g, width)] = jnp.exp2((scores[:, g : g + width] - top) * scale).astype(BF16)

    def sums_of(at, blocks, before, after, i, p):
        reach, near = pl.ds(at * held, blocks * held), pl.ds(0, blocks * held)
        rows, both = rows_of(i), pl.ds(width, 2 * width)
        gained = dot(weight[p][:, near], values[reach, :])
        if before is not None:
            fade = fades[p][...]
            gained = gained + before[rows, both] * jnp.concatenate([fade, fade], axis=1)
        after[rows, both] = gained

    line = []

    def advance(entry):
        n = len(line)
        if n >= 2 and line[n - 2]:
            sums_of(*line[n - 2], n % 2)
        if n >= 1 and line[n - 1]:
            weights_of(*line[n - 1], (n - 1) % 2)
        line.append(entry)
        if entry:
            scores_of(*entry, n % 2)

    def attend(names, before, after):
        first_slot = slot[names[0]] + 1 if names else 0
        blocks = max(len(names), 1)
        if names:
            project(far[pl.ds((first_slot - 1) * held, blocks * held), :], first_slot, blocks)
        else:
            project(clusters[...], 0, 1)
        for i in range(steps):
            advance((first_slot, blocks, before, after, i))

    own_w, sender_w = pl.ds(0, width), pl.ds(width, width)
    attend((), None, first)
    table[pl.ds(0, count), :] = dot(nodes[...], wei[sender_w, :])
    receiver[...] = dot(nodes[...], wei[own_w, :])
    ctable[...] = dot(clusters[...], wni[pl.ds(3 * width, width), :])
    relay_x()
    arrive("y1", "y2", "y3")
    attend(("y1", "y2", "y3"), first, lines.at[0])
    relay_z()
    arrive("z-1", "z1")
    attend(("z-1", "z1", "z-2", "z2"), first, lines.at[1])
    for i in range(len(halo)):
        arrive(f"h{i}")
    table[pl.ds(count, 6 * bound), :] = dot(faces[...], wei[sender_w, :])

    degree = senders.shape[0] * senders.shape[1] // count
    lanes = senders.shape[1]
    part = lanes // degree

    def pick(i, carry):
        start = pl.multiple_of(i * part, part)
        for k in range(part):
            for j in range(degree):
                planes[j, pl.ds(start + k, 1), :] = table[pl.ds(senders[i, k * degree + j], 1), :]
            planes[degree, pl.ds(start + k, 1), :] = ctable[pl.ds(members[start + k], 1), :]
        return carry

    with jax.named_scope("gather"):
        lax.fori_loop(0, senders.shape[0], pick, 0)

    w_out = weo[...]
    w_outs = jnp.concatenate([w_out] * degree, axis=0)

    def edges(i, carry):
        rows = pl.ds(pl.multiple_of(i * BIG, BIG), BIG)
        to = receiver[rows, :]
        hidden = jnp.concatenate([silu(planes[j, rows, :] + to).astype(BF16) for j in range(degree)], axis=1)
        aggregated = dot(hidden, w_outs).astype(BF16)
        mixed = jnp.concatenate([nodes[rows, :], aggregated], axis=1)
        base[rows, :] = dot(mixed, wni[pl.ds(0, 2 * width), :]) + planes[degree, rows, :]
        return carry

    with jax.named_scope("edges"):
        lax.fori_loop(0, count // BIG, edges, 0)

    arrive("r-1", "r1", "r2")
    attend(("x", "r-1", "r1", "r2"), first, lines.at[2])
    arrive("xr-1", "xr1", "xr2")
    attend(("xr-1", "xr1", "xr2"), lines.at[2], lines.at[2])
    arrive("z-3", "z3", "z4_0", f"z4_{held // 2}")
    attend(("z-3", "z3", "z4"), lines.at[1], lines.at[1])
    advance(None)
    advance(None)

    eps_pool, eps_norm = 1e-06, 1e-05

    def finish(i, carry):
        rows = pl.ds(pl.multiple_of(i * BIG, BIG), BIG)
        pooled = jnp.zeros((BIG, width), F32)
        for which in range(3):
            pooled = pooled + lines[which, rows, pl.ds(width, width)] / lines[which, rows, pl.ds(2 * width, width)]
        attended = (pooled * lax.rsqrt(jnp.mean(pooled * pooled, axis=1, keepdims=True) + eps_pool)).astype(BF16)
        preact = dot(attended, wni[pl.ds(2 * width, width), :]) + base[rows, :]
        update = dot(silu(preact).astype(BF16), wno[...])
        centred = update - jnp.mean(update, axis=1, keepdims=True)
        variance = jnp.mean(centred * centred, axis=1, keepdims=True)
        normed = centred * lax.rsqrt(variance + eps_norm)
        out_v[rows, :] = (nodes[rows, :].astype(F32) + normed * gain[...]).astype(BF16)
        return carry

    with jax.named_scope("finish"):
        lax.fori_loop(0, count // BIG, finish, 0)
    copy = pltpu.make_async_copy(out_v, out_h, out_sem)
    copy.start()
    with jax.named_scope("end"):
        for sent in copies.values():
            sent.wait_send()
        copy.wait()


def on_device(mesh, *args):
    nodes, clusters, senders, members, wk, wv, wei, weo, wni, wno, gain = args
    count, width = nodes.shape
    held = clusters.shape[0]
    bound = count // 2
    copies = sum(mesh.shape[a] - 1 for a in ("gx", "gy", "gz"))
    degree = senders.size // count
    hbm = pl.BlockSpec(memory_space=pl.ANY)
    vmem = lambda a: pltpu.VMEM(a.shape, a.dtype)
    gain = gain.reshape(1, width)
    return pl.pallas_call(
        kernel,
        out_shape=jax.ShapeDtypeStruct((count, width), BF16),
        in_specs=[hbm] * 11,
        out_specs=hbm,
        scratch_shapes=[
            pltpu.SMEM(senders.shape, senders.dtype),
            pltpu.SMEM(members.shape, members.dtype),
            *(vmem(a) for a in (nodes, clusters, wk, wv, wei, weo, wni, wno, gain)),
            pltpu.VMEM((copies * held, width), BF16),
            pltpu.VMEM((6 * bound, width), BF16),
            pltpu.VMEM((count + 6 * bound, width), F32),
            pltpu.VMEM((held, width), F32),
            pltpu.VMEM((degree + 1, count, width), F32),
            pltpu.VMEM(((copies + 1) * held, width), BF16),
            pltpu.VMEM(((copies + 1) * held, 2 * width), BF16),
            pltpu.VMEM((count, 3 * width), F32),
            pltpu.VMEM((3, count, 3 * width), F32),
            pltpu.VMEM((count, width), F32),
            pltpu.VMEM((count, width), F32),
            pltpu.VMEM((count, width), BF16),
            *[pltpu.VMEM((ROWS, 4 * held), F32)] * 2,
            *[pltpu.VMEM((ROWS, 4 * held), BF16)] * 2,
            *[pltpu.VMEM((ROWS, width), F32)] * 2,
            pltpu.SemaphoreType.DMA((11,)),
            pltpu.SemaphoreType.DMA((7 + copies,)),
            pltpu.SemaphoreType.DMA((7 + copies,)),
            pltpu.SemaphoreType.DMA,
        ],
        compiler_params=pltpu.CompilerParams(collective_id=0, has_side_effects=True),
        name="layer",
    )(nodes, clusters, senders, members, wk, wv, wei, weo, wni, wno, gain)


def solution(mesh):
    blocks = ("gx", "gy", "gz")
    in_specs = (P(blocks, None), P(blocks, None), P(blocks, None), P(blocks)) + (P(),) * 7
    return jax.shard_map(
        functools.partial(on_device, mesh),
        mesh=mesh, in_specs=in_specs, out_specs=P(blocks, None), check_vma=False,
    )
```

time: 37.4 us -> 34.4 us (0.920)
  Pallas kernels: 35.5 us -> 32.6 us
    pallas_call x1, Pallas kernels: 35.5 us -> 32.6 us  [on_device(): pl.pallas_call(kernel, out_shape=jax.ShapeDtypeStruct((count, width), BF1...]
where the time goes in v3:
time: 34.4 us; the launch traced here: 34.3 us
  Pallas kernels  32.6 us (95%)
  local copies, waits for them, and re-layouts  1.67 us (5%)
    pallas_call x1, Pallas kernels, on_device(): pl.pallas_call(kernel, out_shape=jax.ShapeDtypeStruct((count, width), BF1...  32.6 us
    unnamed x1, local copies, waits for them, and re-layouts  1.67 us

profile of v3, /device:TPU:2, one launch (start us, length us, event | category | flops | bytes accessed | tf_op | source)
XLA Modules:
  0.0 34.3 jit_solution(9204634392959146083)
XLA Ops:
  0.0 32.6 %layer.1 = bf16[1024,128]{1,0:T(8,128)(2,1)} custom-call(bf16[1024,128]{1,0:T(8,128)(2,1)} %nodes_h.1, bf16[256,128]{1,0:T(8,128)(2,1)} %clusters_h.1, s32[32,128]{1,0:T(8,128)} %senders_h.1, s32[1024]{0:T(1024)} %members_h.1, bf16[128,128]{1,0:T(8,128)(2,1)} %wk_h.1, bf16[128,128]{1,0:T(8,128)(2,1)} %wv_h.1, bf16[256,128]{1,0:T(8,128)(2,1)} %wei_h.1, ...), custom_call_target="tpu_custom_call" | custom-call | tf_op jit(solution)/shard_map/layer/pallas_call | solution.py:291
  32.6 1.7 %copy.13 = bf16[1024,128]{1,0:T(8,128)(2,1)} copy(bf16[1024,128]{1,0:T(8,128)(2,1)} %layer.1) | data formatting | bytes 524288

commit v4 on v3

--- a/solution.py
+++ b/solution.py
@@ -13,6 +13,7 @@
 BF16 = jnp.bfloat16
 ROWS = 256
 BIG = 512
+PAD = 8
 NT = (((1,), (1,)), ((), ()))
 
 
@@ -30,7 +31,7 @@
     out_h,
     senders, members, nodes, clusters, wk, wv, wei, weo, wni, wno, gain,
     far, faces, table, ctable, planes, keys, values, first, lines, receiver, base, out_v,
-    score_a, score_b, weight_a, weight_b, fade_a, fade_b,
+    score_a, score_b,
     load_sem, send_sem, recv_sem, out_sem,
 ):
     count, width = nodes.shape
@@ -43,8 +44,10 @@
     half = ny_ring = nx // 2
     upper, ring = lax.div(gx, ny_ring), lax.rem(gx, ny_ring)
 
-    def to_gy(d):
-        return {"gy": lax.rem(gy + d % ny, ny)}
+    core = gy + 1 - 2 * lax.rem(gy, 2)
+    side = lax.rem(gy + ny // 2, ny)
+    diagonal = lax.rem(core + ny // 2, ny)
+    to_gy = {"core": {"gy": core}, "side": {"gy": side}, "diag": {"gy": diagonal}}
 
     def to_gz(d):
         return {"gz": lax.rem(gz + d % nz, nz)}
@@ -56,8 +59,8 @@
         return {"gx": upper * ny_ring + lax.rem(ring + d % ny_ring, ny_ring)}
 
     across = {"gx": lax.rem(gx + half, nx)}
-    halo = [to_gx(1), to_gx(-1), to_gy(1), to_gy(-1), to_gz(1), to_gz(-1)]
-    partners = [to_gy(d) for d in (1, 2, 3)] + [to_gz(d) for d in (1, -1, 2, -2)]
+    halo = [to_gx(1), to_gx(-1), {"gy": lax.rem(gy + 1, ny)}, {"gy": lax.rem(gy + ny - 1, ny)}, to_gz(1), to_gz(-1)]
+    partners = [*to_gy.values()] + [to_gz(d) for d in (1, -1, 2, -2)]
     partners += [across] + [to_ring(d) for d in (1, -1, 2)] + [to_gx(1), to_gx(-1)]
 
     barrier = pltpu.get_barrier_semaphore()
@@ -82,8 +85,8 @@
     with jax.named_scope("barrier_wait"):
         pl.semaphore_wait(barrier, len(partners))
 
-    slots = ["y1", "y2", "y3", "z-1", "z1", "z-2", "z2", "z-3", "z3", "z4"]
-    slots += ["x", "r-1", "r1", "r2", "xr-1", "xr1", "xr2"]
+    slots = ["core", "side", "diag", "z-1", "z1", "z-2", "z2", "z-3", "z3", "z4"]
+    slots += ["r-1", "r1", "x", "r2", "xr-1", "xr1", "xr2"]
     slot = {name: i for i, name in enumerate(slots)}
     copies = {}
 
@@ -98,18 +101,19 @@
     def cell(name, start=0, size=held):
         return far.at[pl.ds(slot[name] * held + start, size)]
 
+    send("core", clusters, cell("core"), to_gy["core"])
     send("x", clusters, cell("x"), across)
-    send("z-2", clusters, cell("z-2"), to_gz(2))
-    send("z2", clusters, cell("z2"), to_gz(-2))
-    for d in (1, 2, 3):
-        send(f"y{d}", clusters, cell(f"y{d}"), to_gy(-d))
     send("z-1", clusters, cell("z-1"), to_gz(1))
     send("z1", clusters, cell("z1"), to_gz(-1))
     send("r-1", clusters, cell("r-1"), to_ring(1))
     send("r1", clusters, cell("r1"), to_ring(-1))
+    send("side", clusters, cell("side"), to_gy["side"])
+    send("diag", clusters, cell("diag"), to_gy["diag"])
     border = nodes.at[pl.ds(0, bound)]
     for i, device in enumerate(halo):
         send(f"h{i}", border, faces.at[pl.ds(i * bound, bound)], device)
+    send("z-2", clusters, cell("z-2"), to_gz(2))
+    send("z2", clusters, cell("z2"), to_gz(-2))
     send("r2", clusters, cell("r2"), to_ring(2))
 
     def arrive(*names):
@@ -134,16 +138,16 @@
         copy.wait()
 
     w_kv = jnp.concatenate([wk[...], wv[...]], axis=1)
-    values[:, pl.ds(width, width)] = jnp.ones((values.shape[0], width), BF16)
+    values[:, pl.ds(width, width)] = jnp.ones((values.shape[0], width), F32)
 
     def project(block, at, blocks):
         both = dot(block, w_kv)
         rows = pl.ds(at * held, blocks * held)
         keys[rows, :] = both[:, :width].astype(BF16)
-        values[rows, pl.ds(0, width)] = both[:, width:].astype(BF16)
+        values[rows, pl.ds(0, width)] = both[:, width:].astype(BF16).astype(F32)
 
     steps = count // ROWS
-    score, weight, fades = (score_a, score_b), (weight_a, weight_b), (fade_a, fade_b)
+    score = (score_a, score_b)
 
     def rows_of(i):
         return pl.ds(i * ROWS, ROWS)
@@ -152,9 +156,9 @@
         reach, near = pl.ds(at * held, blocks * held), pl.ds(0, blocks * held)
         score[p][:, near] = lax.dot_general(nodes[rows_of(i), :], keys[reach, :], NT, preferred_element_type=F32)
 
-    def weights_of(at, blocks, before, after, i, p):
+    def sums_of(at, blocks, before, after, i, p):
         span = blocks * held
-        rows = rows_of(i)
+        rows, both = rows_of(i), pl.ds(width, 2 * width)
         scores = score[p][:, pl.ds(0, span)]
         top = jnp.max(scores, axis=1, keepdims=True)
         if before is None:
@@ -162,17 +166,11 @@
         else:
             old = before[rows, pl.ds(0, width)]
             top = jnp.maximum(old, top)
-            fades[p][...] = jnp.exp2((old - top) * scale)
+            fade = jnp.exp2((old - top) * scale)
         after[rows, pl.ds(0, width)] = top
-        for g in range(0, span, width):
-            weight[p][:, pl.ds(g, width)] = jnp.exp2((scores[:, g : g + width] - top) * scale).astype(BF16)
-
-    def sums_of(at, blocks, before, after, i, p):
-        reach, near = pl.ds(at * held, blocks * held), pl.ds(0, blocks * held)
-        rows, both = rows_of(i), pl.ds(width, 2 * width)
-        gained = dot(weight[p][:, near], values[reach, :])
+        weight = [jnp.exp2((scores[:, g : g + width] - top) * scale) for g in range(0, span, width)]
+        gained = dot(jnp.concatenate(weight, axis=1), values[pl.ds(at * held, span), :])
         if before is not None:
-            fade = fades[p][...]
             gained = gained + before[rows, both] * jnp.concatenate([fade, fade], axis=1)
         after[rows, both] = gained
 
@@ -180,15 +178,13 @@
 
     def advance(entry):
         n = len(line)
-        if n >= 2 and line[n - 2]:
-            sums_of(*line[n - 2], n % 2)
-        if n >= 1 and line[n - 1]:
-            weights_of(*line[n - 1], (n - 1) % 2)
         line.append(entry)
         if entry:
             scores_of(*entry, n % 2)
-
-    def attend(names, before, after):
+        if n >= 1:
+            sums_of(*line[n - 1], (n - 1) % 2)
+
+    def attend(names, before, after, fill=None):
         first_slot = slot[names[0]] + 1 if names else 0
         blocks = max(len(names), 1)
         if names:
@@ -197,65 +193,84 @@
             project(clusters[...], 0, 1)
         for i in range(steps):
             advance((first_slot, blocks, before, after, i))
+            if fill is not None:
+                fill(i)
 
     own_w, sender_w = pl.ds(0, width), pl.ds(width, width)
     attend((), None, first)
-    table[pl.ds(0, count), :] = dot(nodes[...], wei[sender_w, :])
+    table[pl.ds(PAD, count), :] = dot(nodes[...], wei[sender_w, :])
     receiver[...] = dot(nodes[...], wei[own_w, :])
-    ctable[...] = dot(clusters[...], wni[pl.ds(3 * width, width), :])
+    for padded in (table, ctable):
+        padded[pl.ds(0, PAD), :] = jnp.zeros((PAD, width), F32)
+        padded[pl.ds(padded.shape[0] - PAD, PAD), :] = jnp.zeros((PAD, width), F32)
+    ctable[pl.ds(PAD, held), :] = dot(clusters[...], wni[pl.ds(3 * width, width), :])
+    arrive("core")
+    attend(("core",), first, lines.at[0])
+    arrive("z-1", "z1")
+    attend(("z-1", "z1"), first, lines.at[1])
     relay_x()
-    arrive("y1", "y2", "y3")
-    attend(("y1", "y2", "y3"), first, lines.at[0])
-    relay_z()
-    arrive("z-1", "z1")
-    attend(("z-1", "z1", "z-2", "z2"), first, lines.at[1])
-    for i in range(len(halo)):
-        arrive(f"h{i}")
-    table[pl.ds(count, 6 * bound), :] = dot(faces[...], wei[sender_w, :])
+    arrive("r-1", "r1")
+    attend(("r-1", "r1"), first, lines.at[2])
+    arrive("side", "diag")
+    attend(("side", "diag"), lines.at[0], lines.at[0])
 
     degree = senders.shape[0] * senders.shape[1] // count
     lanes = senders.shape[1]
     part = lanes // degree
 
-    def pick(i, carry):
-        start = pl.multiple_of(i * part, part)
-        for k in range(part):
+    sublane = lax.broadcasted_iota(jnp.int32, (PAD, width), 0)
+
+    def pick_rows(source, places):
+        rows = None
+        for k, place in enumerate(places):
+            loaded = source[pl.ds(place + (PAD - k), PAD), :]
+            rows = loaded if rows is None else jnp.where(sublane == k, loaded, rows)
+        return rows
+
+    def pick(i):
+        for start in range(i * part, i * part + part, PAD):
+            ends = range(start, start + PAD)
             for j in range(degree):
-                planes[j, pl.ds(start + k, 1), :] = table[pl.ds(senders[i, k * degree + j], 1), :]
-            planes[degree, pl.ds(start + k, 1), :] = ctable[pl.ds(members[start + k], 1), :]
-        return carry
-
-    with jax.named_scope("gather"):
-        lax.fori_loop(0, senders.shape[0], pick, 0)
+                flat = [n * degree + j for n in ends]
+                planes[j, pl.ds(start, PAD), :] = pick_rows(table, [senders[f // lanes, f % lanes] for f in flat])
+            planes[degree, pl.ds(start, PAD), :] = pick_rows(ctable, [members[n] for n in ends])
+
+    def picks(begin, each):
+        def fill(i):
+            for m in range(begin + i * each, begin + i * each + each):
+                pick(m)
+
+        return fill
 
     w_out = weo[...]
     w_outs = jnp.concatenate([w_out] * degree, axis=0)
 
-    def edges(i, carry):
-        rows = pl.ds(pl.multiple_of(i * BIG, BIG), BIG)
+    def edges(i):
+        rows = rows_of(i)
         to = receiver[rows, :]
         hidden = jnp.concatenate([silu(planes[j, rows, :] + to).astype(BF16) for j in range(degree)], axis=1)
         aggregated = dot(hidden, w_outs).astype(BF16)
         mixed = jnp.concatenate([nodes[rows, :], aggregated], axis=1)
         base[rows, :] = dot(mixed, wni[pl.ds(0, 2 * width), :]) + planes[degree, rows, :]
-        return carry
-
-    with jax.named_scope("edges"):
-        lax.fori_loop(0, count // BIG, edges, 0)
-
-    arrive("r-1", "r1", "r2")
-    attend(("x", "r-1", "r1", "r2"), first, lines.at[2])
+
+    for i in range(len(halo)):
+        arrive(f"h{i}")
+    table[pl.ds(PAD + count, 6 * bound), :] = dot(faces[...], wei[sender_w, :])
+    each = senders.shape[0] // (2 * steps)
+    relay_z()
+    arrive("r2")
+    attend(("x", "r2"), lines.at[2], lines.at[2], picks(0, each))
     arrive("xr-1", "xr1", "xr2")
-    attend(("xr-1", "xr1", "xr2"), lines.at[2], lines.at[2])
+    attend(("xr-1", "xr1", "xr2"), lines.at[2], lines.at[2], picks(steps * each, each))
+    attend(("z-2", "z2"), lines.at[1], lines.at[1], edges)
     arrive("z-3", "z3", "z4_0", f"z4_{held // 2}")
     attend(("z-3", "z3", "z4"), lines.at[1], lines.at[1])
     advance(None)
-    advance(None)
 
     eps_pool, eps_norm = 1e-06, 1e-05
 
     def finish(i, carry):
-        rows = pl.ds(pl.multiple_of(i * BIG, BIG), BIG)
+        rows = pl.ds(i * BIG, BIG)
         pooled = jnp.zeros((BIG, width), F32)
         for which in range(3):
             pooled = pooled + lines[which, rows, pl.ds(width, width)] / lines[which, rows, pl.ds(2 * width, width)]
@@ -268,14 +283,18 @@
         out_v[rows, :] = (nodes[rows, :].astype(F32) + normed * gain[...]).astype(BF16)
         return carry
 
+    pieces = []
     with jax.named_scope("finish"):
-        lax.fori_loop(0, count // BIG, finish, 0)
-    copy = pltpu.make_async_copy(out_v, out_h, out_sem)
-    copy.start()
+        for i in range(count // BIG):
+            finish(i, 0)
+            rows = pl.ds(i * BIG, BIG)
+            pieces.append(pltpu.make_async_copy(out_v.at[rows], out_h.at[rows], out_sem.at[i]))
+            pieces[-1].start()
     with jax.named_scope("end"):
         for sent in copies.values():
             sent.wait_send()
-        copy.wait()
+        for copy in pieces:
+            copy.wait()
 
 
 def on_device(mesh, *args):
@@ -299,23 +318,21 @@
             *(vmem(a) for a in (nodes, clusters, wk, wv, wei, weo, wni, wno, gain)),
             pltpu.VMEM((copies * held, width), BF16),
             pltpu.VMEM((6 * bound, width), BF16),
-            pltpu.VMEM((count + 6 * bound, width), F32),
-            pltpu.VMEM((held, width), F32),
+            pltpu.VMEM((count + 6 * bound + 2 * PAD, width), F32),
+            pltpu.VMEM((held + 2 * PAD, width), F32),
             pltpu.VMEM((degree + 1, count, width), F32),
             pltpu.VMEM(((copies + 1) * held, width), BF16),
-            pltpu.VMEM(((copies + 1) * held, 2 * width), BF16),
+            pltpu.VMEM(((copies + 1) * held, 2 * width), F32),
             pltpu.VMEM((count, 3 * width), F32),
             pltpu.VMEM((3, count, 3 * width), F32),
             pltpu.VMEM((count, width), F32),
             pltpu.VMEM((count, width), F32),
             pltpu.VMEM((count, width), BF16),
             *[pltpu.VMEM((ROWS, 4 * held), F32)] * 2,
-            *[pltpu.VMEM((ROWS, 4 * held), BF16)] * 2,
-            *[pltpu.VMEM((ROWS, width), F32)] * 2,
             pltpu.SemaphoreType.DMA((11,)),
             pltpu.SemaphoreType.DMA((7 + copies,)),
             pltpu.SemaphoreType.DMA((7 + copies,)),
-            pltpu.SemaphoreType.DMA,
+            pltpu.SemaphoreType.DMA((count // BIG,)),
         ],
         compiler_params=pltpu.CompilerParams(collective_id=0, has_side_effects=True),
         name="layer",

time: 34.4 us -> 31.4 us (0.913)
  Pallas kernels: 32.6 us -> 29.4 us
    pallas_call x1, Pallas kernels: 32.6 us -> 29.4 us  [on_device(): pl.pallas_call(kernel, out_shape=jax.ShapeDtypeStruct((count, width), BF1...]
where the time goes in v4:
time: 31.4 us; the launch traced here: 31.1 us
  Pallas kernels  29.4 us (94%)
  local copies, waits for them, and re-layouts  1.67 us (5%)
    pallas_call x1, Pallas kernels, on_device(): pl.pallas_call(kernel, out_shape=jax.ShapeDtypeStruct((count, width), BF1...  29.4 us
    unnamed x1, local copies, waits for them, and re-layouts  1.67 us

profile of v4, /device:TPU:2, one launch (start us, length us, event | category | flops | bytes accessed | tf_op | source)
XLA Modules:
  0.0 31.1 jit_solution(5456051952968252449)
XLA Ops:
  0.0 29.4 %layer.1 = bf16[1024,128]{1,0:T(8,128)(2,1)} custom-call(bf16[1024,128]{1,0:T(8,128)(2,1)} %nodes_h.1, bf16[256,128]{1,0:T(8,128)(2,1)} %clusters_h.1, s32[32,128]{1,0:T(8,128)} %senders_h.1, s32[1024]{0:T(1024)} %members_h.1, bf16[128,128]{1,0:T(8,128)(2,1)} %wk_h.1, bf16[128,128]{1,0:T(8,128)(2,1)} %wv_h.1, bf16[256,128]{1,0:T(8,128)(2,1)} %wei_h.1, ...), custom_call_target="tpu_custom_call" | custom-call | tf_op jit(solution)/shard_map/layer/pallas_call | solution.py:310
  29.4 1.7 %copy.13 = bf16[1024,128]{1,0:T(8,128)(2,1)} copy(bf16[1024,128]{1,0:T(8,128)(2,1)} %layer.1) | data formatting | bytes 524288

commit v5 on v4

--- a/solution.py
+++ b/solution.py
@@ -101,6 +101,7 @@
     def cell(name, start=0, size=held):
         return far.at[pl.ds(slot[name] * held + start, size)]
 
+    border = nodes.at[pl.ds(0, bound)]
     send("core", clusters, cell("core"), to_gy["core"])
     send("x", clusters, cell("x"), across)
     send("z-1", clusters, cell("z-1"), to_gz(1))
@@ -109,11 +110,14 @@
     send("r1", clusters, cell("r1"), to_ring(-1))
     send("side", clusters, cell("side"), to_gy["side"])
     send("diag", clusters, cell("diag"), to_gy["diag"])
-    border = nodes.at[pl.ds(0, bound)]
-    for i, device in enumerate(halo):
-        send(f"h{i}", border, faces.at[pl.ds(i * bound, bound)], device)
     send("z-2", clusters, cell("z-2"), to_gz(2))
     send("z2", clusters, cell("z2"), to_gz(-2))
+    send("h0", border, faces.at[pl.ds(0 * bound, bound)], halo[0])
+    send("h1", border, faces.at[pl.ds(1 * bound, bound)], halo[1])
+    send("h2", border, faces.at[pl.ds(2 * bound, bound)], halo[2])
+    send("h3", border, faces.at[pl.ds(3 * bound, bound)], halo[3])
+    send("h4", border, faces.at[pl.ds(4 * bound, bound)], halo[4])
+    send("h5", border, faces.at[pl.ds(5 * bound, bound)], halo[5])
     send("r2", clusters, cell("r2"), to_ring(2))
 
     def arrive(*names):
@@ -197,6 +201,50 @@
                 fill(i)
 
     own_w, sender_w = pl.ds(0, width), pl.ds(width, width)
+    degree = senders.shape[0] * senders.shape[1] // count
+    lanes = senders.shape[1]
+    part = lanes // degree
+
+    sublane = lax.broadcasted_iota(jnp.int32, (PAD, width), 0)
+
+    def pick_rows(source, places):
+        rows = None
+        for k, place in enumerate(places):
+            loaded = source[pl.ds(place + (PAD - k), PAD), :]
+            rows = loaded if rows is None else jnp.where(sublane == k, loaded, rows)
+        return rows
+
+    def pick(i):
+        for start in range(i * part, i * part + part, PAD):
+            ends = range(start, start + PAD)
+            for j in range(degree):
+                flat = [n * degree + j for n in ends]
+                planes[j, pl.ds(start, PAD), :] = pick_rows(table, [senders[f // lanes, f % lanes] for f in flat])
+
+    def pick_own(i, carry):
+        start = pl.multiple_of(i * part, part)
+        for n in range(0, part, PAD):
+            own = pick_rows(ctable, [members[start + n + k] for k in range(PAD)])
+            base[pl.ds(start + n, PAD), :] = base[pl.ds(start + n, PAD), :] + own
+        return carry
+
+    def picks(begin, each):
+        def fill(i):
+            for m in range(begin + i * each, begin + i * each + each):
+                pick(m)
+
+        return fill
+
+    w_out = weo[...]
+    w_outs = jnp.concatenate([w_out] * degree, axis=0)
+
+    def edges(i):
+        rows = rows_of(i)
+        to = receiver[rows, :]
+        hidden = jnp.concatenate([silu(planes[j, rows, :] + to).astype(BF16) for j in range(degree)], axis=1)
+        aggregated = dot(hidden, w_outs).astype(BF16)
+        base[rows, :] = base[rows, :] + dot(aggregated, wni[pl.ds(width, width), :])
+
     attend((), None, first)
     table[pl.ds(PAD, count), :] = dot(nodes[...], wei[sender_w, :])
     receiver[...] = dot(nodes[...], wei[own_w, :])
@@ -204,8 +252,11 @@
         padded[pl.ds(0, PAD), :] = jnp.zeros((PAD, width), F32)
         padded[pl.ds(padded.shape[0] - PAD, PAD), :] = jnp.zeros((PAD, width), F32)
     ctable[pl.ds(PAD, held), :] = dot(clusters[...], wni[pl.ds(3 * width, width), :])
+    base[...] = dot(nodes[...], wni[pl.ds(0, width), :])
     arrive("core")
     attend(("core",), first, lines.at[0])
+    with jax.named_scope("members"):
+        lax.fori_loop(0, count // part, pick_own, 0)
     arrive("z-1", "z1")
     attend(("z-1", "z1"), first, lines.at[1])
     relay_x()
@@ -213,58 +264,18 @@
     attend(("r-1", "r1"), first, lines.at[2])
     arrive("side", "diag")
     attend(("side", "diag"), lines.at[0], lines.at[0])
-
-    degree = senders.shape[0] * senders.shape[1] // count
-    lanes = senders.shape[1]
-    part = lanes // degree
-
-    sublane = lax.broadcasted_iota(jnp.int32, (PAD, width), 0)
-
-    def pick_rows(source, places):
-        rows = None
-        for k, place in enumerate(places):
-            loaded = source[pl.ds(place + (PAD - k), PAD), :]
-            rows = loaded if rows is None else jnp.where(sublane == k, loaded, rows)
-        return rows
-
-    def pick(i):
-        for start in range(i * part, i * part + part, PAD):
-            ends = range(start, start + PAD)
-            for j in range(degree):
-                flat = [n * degree + j for n in ends]
-                planes[j, pl.ds(start, PAD), :] = pick_rows(table, [senders[f // lanes, f % lanes] for f in flat])
-            planes[degree, pl.ds(start, PAD), :] = pick_rows(ctable, [members[n] for n in ends])
-
-    def picks(begin, each):
-        def fill(i):
-            for m in range(begin + i * each, begin + i * each + each):
-                pick(m)
-
-        return fill
-
-    w_out = weo[...]
-    w_outs = jnp.concatenate([w_out] * degree, axis=0)
-
-    def edges(i):
-        rows = rows_of(i)
-        to = receiver[rows, :]
-        hidden = jnp.concatenate([silu(planes[j, rows, :] + to).astype(BF16) for j in range(degree)], axis=1)
-        aggregated = dot(hidden, w_outs).astype(BF16)
-        mixed = jnp.concatenate([nodes[rows, :], aggregated], axis=1)
-        base[rows, :] = dot(mixed, wni[pl.ds(0, 2 * width), :]) + planes[degree, rows, :]
-
+    relay_z()
+    attend(("z-2", "z2"), lines.at[1], lines.at[1])
     for i in range(len(halo)):
         arrive(f"h{i}")
     table[pl.ds(PAD + count, 6 * bound), :] = dot(faces[...], wei[sender_w, :])
     each = senders.shape[0] // (2 * steps)
-    relay_z()
     arrive("r2")
     attend(("x", "r2"), lines.at[2], lines.at[2], picks(0, each))
     arrive("xr-1", "xr1", "xr2")
     attend(("xr-1", "xr1", "xr2"), lines.at[2], lines.at[2], picks(steps * each, each))
-    attend(("z-2", "z2"), lines.at[1], lines.at[1], edges)
     arrive("z-3", "z3", "z4_0", f"z4_{held // 2}")
-    attend(("z-3", "z3", "z4"), lines.at[1], lines.at[1])
+    attend(("z-3", "z3", "z4"), lines.at[1], lines.at[1], edges)
     advance(None)
 
     eps_pool, eps_norm = 1e-06, 1e-05
@@ -320,7 +331,7 @@
             pltpu.VMEM((6 * bound, width), BF16),
             pltpu.VMEM((count + 6 * bound + 2 * PAD, width), F32),
             pltpu.VMEM((held + 2 * PAD, width), F32),
-            pltpu.VMEM((degree + 1, count, width), F32),
+            pltpu.VMEM((degree, count, width), F32),
             pltpu.VMEM(((copies + 1) * held, width), BF16),
             pltpu.VMEM(((copies + 1) * held, 2 * width), F32),
             pltpu.VMEM((count, 3 * width), F32),

time: 31.4 us -> 30 us (0.955)
  Pallas kernels: 29.4 us -> 28.2 us
    pallas_call x1, Pallas kernels: 29.4 us -> 28.2 us  [on_device(): pl.pallas_call(kernel, out_shape=jax.ShapeDtypeStruct((count, width), BF1...]
where the time goes in v5:
time: 30 us; the launch traced here: 29.9 us
  Pallas kernels  28.2 us (94%)
  local copies, waits for them, and re-layouts  1.67 us (6%)
    pallas_call x1, Pallas kernels, on_device(): pl.pallas_call(kernel, out_shape=jax.ShapeDtypeStruct((count, width), BF1...  28.2 us
    unnamed x1, local copies, waits for them, and re-layouts  1.67 us

profile of v5, /device:TPU:2, one launch (start us, length us, event | category | flops | bytes accessed | tf_op | source)
XLA Modules:
  0.0 29.9 jit_solution(10719418811276176447)
XLA Ops:
  0.0 28.2 %layer.1 = bf16[1024,128]{1,0:T(8,128)(2,1)} custom-call(bf16[1024,128]{1,0:T(8,128)(2,1)} %nodes_h.1, bf16[256,128]{1,0:T(8,128)(2,1)} %clusters_h.1, s32[32,128]{1,0:T(8,128)} %senders_h.1, s32[1024]{0:T(1024)} %members_h.1, bf16[128,128]{1,0:T(8,128)(2,1)} %wk_h.1, bf16[128,128]{1,0:T(8,128)(2,1)} %wv_h.1, bf16[256,128]{1,0:T(8,128)(2,1)} %wei_h.1, ...), custom_call_target="tpu_custom_call" | custom-call | tf_op jit(solution)/shard_map/layer/pallas_call | solution.py:321
  28.2 1.7 %copy.13 = bf16[1024,128]{1,0:T(8,128)(2,1)} copy(bf16[1024,128]{1,0:T(8,128)(2,1)} %layer.1) | data formatting | bytes 524288

commit v6 on v5

--- a/solution.py
+++ b/solution.py
@@ -261,7 +261,7 @@
     attend(("z-1", "z1"), first, lines.at[1])
     relay_x()
     arrive("r-1", "r1")
-    attend(("r-1", "r1"), first, lines.at[2])
+    attend(("r-1", "r1", "x"), first, lines.at[2])
     arrive("side", "diag")
     attend(("side", "diag"), lines.at[0], lines.at[0])
     relay_z()
@@ -269,13 +269,14 @@
     for i in range(len(halo)):
         arrive(f"h{i}")
     table[pl.ds(PAD + count, 6 * bound), :] = dot(faces[...], wei[sender_w, :])
-    each = senders.shape[0] // (2 * steps)
-    arrive("r2")
-    attend(("x", "r2"), lines.at[2], lines.at[2], picks(0, each))
-    arrive("xr-1", "xr1", "xr2")
-    attend(("xr-1", "xr1", "xr2"), lines.at[2], lines.at[2], picks(steps * each, each))
+    for i in range(senders.shape[0]):
+        pick(i)
+    for i in range(steps):
+        edges(i)
+    arrive("r2", "xr-1", "xr1", "xr2")
+    attend(("r2", "xr-1", "xr1", "xr2"), lines.at[2], lines.at[2])
     arrive("z-3", "z3", "z4_0", f"z4_{held // 2}")
-    attend(("z-3", "z3", "z4"), lines.at[1], lines.at[1], edges)
+    attend(("z-3", "z3", "z4"), lines.at[1], lines.at[1])
     advance(None)
 
     eps_pool, eps_norm = 1e-06, 1e-05

time: 30 us -> 30 us (level)
  no operation moved by 1% of the time
where the time goes in v6:
time: 30 us; the launch traced here: 29.8 us
  Pallas kernels  28.2 us (94%)
  local copies, waits for them, and re-layouts  1.67 us (6%)
    pallas_call x1, Pallas kernels, on_device(): pl.pallas_call(kernel, out_shape=jax.ShapeDtypeStruct((count, width), BF1...  28.2 us
    unnamed x1, local copies, waits for them, and re-layouts  1.67 us

profile of v6, /device:TPU:2, one launch (start us, length us, event | category | flops | bytes accessed | tf_op | source)
XLA Modules:
  0.0 29.8 jit_solution(6734079156914465511)
XLA Ops:
  0.0 28.2 %layer.1 = bf16[1024,128]{1,0:T(8,128)(2,1)} custom-call(bf16[1024,128]{1,0:T(8,128)(2,1)} %nodes_h.1, bf16[256,128]{1,0:T(8,128)(2,1)} %clusters_h.1, s32[32,128]{1,0:T(8,128)} %senders_h.1, s32[1024]{0:T(1024)} %members_h.1, bf16[128,128]{1,0:T(8,128)(2,1)} %wk_h.1, bf16[128,128]{1,0:T(8,128)(2,1)} %wv_h.1, bf16[256,128]{1,0:T(8,128)(2,1)} %wei_h.1, ...), custom_call_target="tpu_custom_call" | custom-call | tf_op jit(solution)/shard_map/layer/pallas_call | solution.py:322
  28.2 1.7 %copy.13 = bf16[1024,128]{1,0:T(8,128)(2,1)} copy(bf16[1024,128]{1,0:T(8,128)(2,1)} %layer.1) | data formatting | bytes 524288
